TPU v7x, 32 devices: a whole 2x2x4 slice. The times are simulated.
32 devices in a mesh: dp: 8 (over z, x), expert: 4 (over y, core).
Axes of the slice: x: 2, y: 2, z: 4, core: 2. Of those that a mesh axis runs over, the one named last changes fastest.
Arguments:
- tokens: bfloat16 [32768, 768], P(('dp', 'expert')), may hold values from -6 to 6
- prev_scores: float32 [32768, 8], P(('dp', 'expert')), may hold values from -6 to 6
- segments: int32 [32, 1024], P(('dp', 'expert')), may hold values from 0 to 7, never falling along the last dimension, each value on 1 to 512 neighbouring positions
- routes: int32 [32768, 2], P(('dp', 'expert')), may hold values from 0 to 7, all different within a row; in each aligned block of 1024 rows (0 to 1023, 1024 to 2047, ...) at most 256 rows name the same one
- wqkv: bfloat16 [768, 2304], P('dp'), may hold values from -0.21875 to 0.21875
- wo: bfloat16 [768, 768], P('dp'), may hold values from -1.75 to 1.75
- router: bfloat16 [768, 8], P('dp'), may hold values from -0.125 to 0.125
- const_gate: bfloat16 [768, 4], P('dp'), may hold values from -0.21875 to 0.21875
- const_vec: bfloat16 [768, 2], P('dp'), may hold values from -5 to 5
- gain1: bfloat16 [768], P('dp'), may hold values from 0.5 to 1.5
- gain2: bfloat16 [768], P('dp'), may hold values from 0.5 to 1.5
- gate_mix: bfloat16 [8, 8], replicated, may hold values from -0.8984375 to 0.8984375
- w_in: bfloat16 [4, 768, 4096], P('expert'), may hold values from -0.21875 to 0.21875
- w_out: bfloat16 [4, 2048, 768], P('expert'), may hold values from -0.125 to 0.125
- cotangent: bfloat16 [32768, 768], P(('dp', 'expert')), may hold values from -6 to 6
Outputs:
- mixed: bfloat16 [32768, 768], P(('dp', 'expert'))
- grad_tokens: float32 [32768, 768], P(('dp', 'expert'))
- grad_prev: float32 [32768, 8], P(('dp', 'expert'))
- grad_wqkv: float32 [768, 2304], P('dp')
- grad_wo: float32 [768, 768], P('dp')
- grad_router: float32 [768, 8], P('dp')
- grad_const_gate: float32 [768, 4], P('dp')
- grad_const_vec: float32 [768, 2], P('dp')
- grad_gain1: float32 [768], P('dp')
- grad_gain2: float32 [768], P('dp')
- grad_gate_mix: float32 [8, 8], replicated
- grad_w_in: float32 [4, 768, 4096], P('expert', 'dp')
- grad_w_out: float32 [4, 2048, 768], P('expert', 'dp')
Inputs may be any that keep to these rules, and one draw needn't show every extreme that they name: `routes`: each token names two different experts. Within the tokens of one device (aligned blocks of 1024 rows), no expert is named by more than 256 tokens, and some expert reaches 256. `segments`: within a sequence the numbers never fall; a document has at most 512 positions, and one has exactly that many.
All inputs are finite; a program needn't handle non-finite values.
Results may differ from a plain program's by a relative error of at most 0.014.
The roundings to bfloat16 on the way count: a program that leaves them out, or rounds other values in their place, can miss the bound.
Values may be sent and summed in bfloat16 or wider, within the bound.
A program may use at most 256 MiB of HBM per device.

v0:
```python
import functools

import jax
import jax.numpy as jnp
from jax import lax
from jax.experimental import pallas as pl
from jax.experimental.pallas import tpu as pltpu
from jax.sharding import PartitionSpec as P


HEADS = 12
HEAD_DIM = 64
CAP = 256
DOC_MAX = 512
NORM_EPSILON = 1e-06
HIGHEST_PRECISION = lax.Precision.HIGHEST
NEGATIVE = -1e30
F32 = jnp.float32
BF16 = jnp.bfloat16
BLOCK = 256
GROUP = 4
GROUP_LANES = GROUP * HEAD_DIM
LANES = 128
MESH = pl.DeviceIdType.MESH
VMEM_BYTES = 62 * 1024 * 1024


def nn(left, right):
    return jnp.dot(left, right, preferred_element_type=F32)


def nt(left, right):
    return lax.dot_general(left, right, (((1,), (1,)), ((), ())), preferred_element_type=F32)


def tn(left, right):
    return lax.dot_general(left, right, (((0,), (0,)), ((), ())), preferred_element_type=F32)


def iota(shape, axis):
    return lax.broadcasted_iota(jnp.int32, shape, axis)


def split_low(values):
    high = values.astype(BF16)
    return high, (values - high.astype(F32)).astype(BF16)


def inverse_rms(values):
    return lax.rsqrt(jnp.mean(values * values, axis=-1, keepdims=True) + NORM_EPSILON)


def norm_back(upstream, normed, inverse):
    return inverse * (upstream - normed * jnp.mean(upstream * normed, axis=-1, keepdims=True))


def turn(values, cosines, signed_sines):
    pieces = []
    for start in range(0, values.shape[1], LANES):
        part = values[:, start : start + LANES]
        front = iota(part.shape, 1) % HEAD_DIM < HEAD_DIM // 2
        swapped = jnp.where(
            front,
            pltpu.roll(part, LANES - HEAD_DIM // 2, 1),
            pltpu.roll(part, HEAD_DIM // 2, 1),
        )
        pieces.append(part * cosines + swapped * signed_sines)
    return jnp.concatenate(pieces, axis=1)


def head_mask(head):
    return (iota((1, GROUP_LANES), 1) // HEAD_DIM == head).astype(F32).astype(BF16)


def params(**extra):
    return pltpu.CompilerParams(vmem_limit_bytes=VMEM_BYTES, **extra)


def whole_block(shape):
    return pl.BlockSpec(shape, lambda *_: (0,) * len(shape))


def cost(flops, moved):
    return pl.CostEstimate(flops=int(flops), bytes_accessed=int(moved), transcendentals=0)


def send_cotangent_kernel(experts, cot_ref, target_ref, out_ref):
    tokens = cot_ref.shape[0]

    @pl.loop(0, experts)
    def _(expert):
        slots = iota((CAP, tokens), 0) + expert * CAP
        hot = (target_ref[0:1, :] == slots) | (target_ref[1:2, :] == slots)
        out_ref[expert] = nn(hot.astype(F32).astype(BF16), cot_ref[...]).astype(BF16)


def attend_kernel(
    gain_row, tok_ref, wq_ref, wk_ref, wv_ref, small_ref, cos_ref, sin_ref, segc_ref, segr_ref,
    qkv_ref, attn_in_ref, out_ref, lse_ref, gain_ref, bias_ref, log_ref,
):
    step = pl.program_id(0)
    tokens = tok_ref.shape[0]
    blocks = tokens // BLOCK
    reach = DOC_MAX // BLOCK

    @pl.when(step == 0)
    def _():
        gain_ref[...] = small_ref[...].astype(F32).T[gain_row : gain_row + 1, :]
        log_ref[...] = jnp.zeros_like(log_ref)

        @pl.loop(0, blocks)
        def _(block):
            rows = pl.ds(pl.multiple_of(block * BLOCK, BLOCK), BLOCK)
            values = tok_ref[rows, :].astype(F32)
            attn_in_ref[rows, :] = (values * inverse_rms(values) * gain_ref[...]).astype(BF16)

    @pl.loop(0, blocks)
    def _(block):
        rows = pl.ds(pl.multiple_of(block * BLOCK, BLOCK), BLOCK)
        normed = attn_in_ref[rows, :]
        cosines = cos_ref[rows, :]
        sines = sin_ref[rows, :]
        query = turn(nn(normed, wq_ref[...]), cosines, sines) * HEAD_DIM**-0.5
        qkv_ref[0, rows, :] = query.astype(BF16)
        qkv_ref[1, rows, :] = turn(nn(normed, wk_ref[...]), cosines, sines).astype(BF16)
        qkv_ref[2, rows, :] = nn(normed, wv_ref[...]).astype(BF16)

    for block in range(blocks):
        first = max(0, block - reach) * BLOCK
        last = (block + 1) * BLOCK
        span = last - first
        rows = slice(block * BLOCK, last)
        row_ids = iota((BLOCK, span), 0) + block * BLOCK
        col_ids = iota((BLOCK, span), 1) + first
        seen = (col_ids <= row_ids) & (segc_ref[rows, :] == segr_ref[0:1, first:last])
        bias_ref[:, 0:span] = jnp.where(seen, 0.0, NEGATIVE)
        attended = []
        logs = log_ref[rows, :]
        for head in range(GROUP):
            mask = head_mask(head)
            scores = nt(qkv_ref[0, rows, :] * mask, qkv_ref[1, first:last, :]) + bias_ref[:, 0:span]
            top = jnp.max(scores, axis=1, keepdims=True)
            weights = jnp.exp(scores - top).astype(BF16)
            value = qkv_ref[2, first:last, :] * mask + (1 - mask)
            mixed = nn(weights, value)
            own = iota(mixed.shape, 1) // HEAD_DIM == head
            total = jnp.max(jnp.where(own, 0.0, mixed), axis=1, keepdims=True)
            attended.append(jnp.where(own, mixed / total, 0.0))
            logs = jnp.where(
                iota(logs.shape, 1) == step * GROUP + head, top + jnp.log(total), logs
            )
        log_ref[rows, :] = logs
        out_ref[rows, :] = (attended[0] + attended[1] + attended[2] + attended[3]).astype(BF16)

    @pl.when(step == pl.num_programs(0) - 1)
    def _():
        lse_ref[...] = log_ref[...].T[0 : lse_ref.shape[0], :]


def middle_kernel(
    kinds, ao_ref, wo_ref, tok_ref, small_ref, prev_ref, routes_ref, target_ref,
    resid_ref, scal_ref, send_ref, ffn_ref, first_ref, second_ref,
):
    tokens, width = tok_ref.shape
    gain = small_ref[...].astype(F32).T[kinds + 7 : kinds + 8, :]

    @pl.loop(0, tokens // BLOCK)
    def _(block):
        rows = pl.ds(pl.multiple_of(block * BLOCK, BLOCK), BLOCK)
        resid = tok_ref[rows, :].astype(F32) + nn(ao_ref[rows, :], wo_ref[...])
        resid_ref[rows, :] = resid
        inverse = inverse_rms(resid)
        low = (resid * inverse * gain).astype(BF16)
        ffn_ref[rows, :] = low
        logits = nn(low, small_ref[...]) + prev_ref[rows, :]
        lane = iota(logits.shape, 1)

        def pick(index):
            return jnp.sum(jnp.where(lane == index, logits, 0.0), axis=1, keepdims=True)

        def pair(left, right):
            top = jnp.maximum(left, right)
            left = jnp.exp(left - top)
            right = jnp.exp(right - top)
            total = left + right
            return left / total, right / total

        gates = pair(pick(routes_ref[rows, 0:1]), pick(routes_ref[rows, 1:2]))
        one = pair(pick(kinds), pick(kinds + 1))
        two = pair(pick(kinds + 2), pick(kinds + 3))
        scal = jnp.zeros_like(logits)
        for index, value in enumerate(gates + one + two + (inverse,)):
            scal = jnp.where(lane == index, value, scal)
        scal_ref[rows, :] = scal
        for gate, ref in zip(gates, (first_ref, second_ref)):
            high, rest = split_low(gate)
            ref[rows, :] = jnp.where(
                lane == 0, high.astype(F32), jnp.where(lane == 1, rest.astype(F32), 0.0)
            ).astype(BF16)

    @pl.loop(0, send_ref.shape[0])
    def _(expert):
        slots = iota((CAP, tokens), 0) + expert * CAP
        hot_one = (target_ref[0:1, :] == slots).astype(F32)
        hot_two = (target_ref[1:2, :] == slots).astype(F32)
        send_ref[expert, :, 0:width] = nn((hot_one + hot_two).astype(BF16), ffn_ref[...]).astype(
            BF16
        )
        send_ref[expert, :, width:] = (
            nn(hot_one.astype(BF16), first_ref[...]) + nn(hot_two.astype(BF16), second_ref[...])
        ).astype(BF16)


def expert_kernel(
    recv_ref, cot_ref, wg_ref, wu_ref, wo_ref, front_ref, ret_ref, out_acc, row_acc,
):
    step = pl.program_id(0)
    total, width = out_acc.shape
    tile = 512

    @pl.when(step == 0)
    def _():
        out_acc[...] = jnp.zeros_like(out_acc)
        row_acc[...] = jnp.zeros_like(row_acc)

    @pl.loop(0, total // tile)
    def _(block):
        rows = pl.ds(pl.multiple_of(block * tile, tile), tile)
        token = recv_ref[rows, 0:width]
        extra = recv_ref[rows, width:].astype(F32)
        gate_weight = extra[:, 0:1] + extra[:, 1:2]
        gate = nn(token, wg_ref[...])
        up = nn(token, wu_ref[...])
        grad = nt(cot_ref[rows, :], wo_ref[...]) * gate_weight
        sig = jax.nn.sigmoid(gate)
        act = gate * sig
        hidden = act * up
        out_acc[rows, :] += nn(hidden.astype(BF16), wo_ref[...])
        front_ref[2, rows, :] = (hidden * gate_weight).astype(BF16)
        gate_grad = (grad * up * sig * (1.0 + gate * (1.0 - sig))).astype(BF16)
        up_grad = (grad * act).astype(BF16)
        front_ref[0, rows, :] = gate_grad
        front_ref[1, rows, :] = up_grad
        row_acc[rows, :] += nt(gate_grad, wg_ref[...]) + nt(up_grad, wu_ref[...])

    @pl.when(step == pl.num_programs(0) - 1)
    def _():
        @pl.loop(0, total // CAP)
        def _(peer):
            rows = pl.ds(pl.multiple_of(peer * CAP, CAP), CAP)
            ret_ref[peer, 0:CAP, :] = out_acc[rows, :].astype(BF16)
            ret_ref[peer, CAP:, :] = row_acc[rows, :].astype(BF16)


def expert_grad_kernel(recv_ref, cot_ref, front_ref, gate_ref, up_ref, wout_ref, turned_ref):
    step = pl.program_id(0)
    width = turned_ref.shape[0]

    @pl.when(step == 0)
    def _():
        turned_ref[...] = recv_ref[:, 0:width].T

    wout_ref[...] = tn(front_ref[2], cot_ref[...]).astype(BF16)
    gate_ref[...] = nn(turned_ref[...], front_ref[0]).astype(BF16)
    up_ref[...] = nn(turned_ref[...], front_ref[1]).astype(BF16)


def combine_kernel(
    kinds, experts, ret_ref, target_ref, routes_ref, scal_ref, resid_ref, cot_ref, ao_ref,
    small_ref, wo_ref, mix_ref, prevt_ref, ind_ref,
    mixed_ref, prev_ref, mid_ref, proj_ref, attn_ref, delta_ref, minor_ref, vec_ref, gain_ref,
    gmix_ref, rows_ref,
):
    step = pl.program_id(0)

    @pl.when(step == 0)
    def _():
        rows_ref[...] = small_ref[...].astype(F32).T
        minor_ref[...] = jnp.zeros_like(minor_ref)
        vec_ref[...] = jnp.zeros_like(vec_ref)
        gain_ref[...] = jnp.zeros_like(gain_ref)
        gmix_ref[...] = jnp.zeros_like(gmix_ref)

    width = resid_ref.shape[1]
    slots = experts * CAP
    resid = resid_ref[...]
    cot = cot_ref[...]
    upstream = cot.astype(F32)
    scal = scal_ref[...]
    routes = (routes_ref[:, 0:1], routes_ref[:, 1:2])
    targets = (target_ref[:, 0:1], target_ref[:, 1:2])
    gates = (scal[:, 0:1], scal[:, 1:2])
    one_keep, one_vec = scal[:, 2:3], scal[:, 3:4]
    two_keep, two_vec = scal[:, 4:5], scal[:, 5:6]
    inverse = scal[:, 6:7]
    gain = rows_ref[kinds + 7 : kinds + 8, :]
    vec_one = rows_ref[kinds + 4 : kinds + 5, :]
    vec_two = rows_ref[kinds + 5 : kinds + 6, :]
    normed = resid * inverse
    ffn_norm = normed * gain
    low = ffn_norm.astype(BF16)
    slot_ids = iota((BLOCK, slots), 1)
    hots = [(target == slot_ids).astype(F32) for target in targets]
    outs = ret_ref[:, 0:CAP, :].reshape(slots, width)
    backs = ret_ref[:, CAP:, :].reshape(slots, width)
    branches = [nn(hot.astype(BF16), outs) for hot in hots]
    back = nn((hots[0] + hots[1]).astype(BF16), backs)

    def weight(kind):
        return sum(
            jnp.where(route == kind, gate, 0.0) for route, gate in zip(routes, gates)
        )

    weight_copy = weight(experts + 1)
    weight_one = weight(experts + 2)
    weight_two = weight(experts + 3)
    keep = weight_copy + weight_one * one_keep + weight_two * two_keep
    mixed_ref[...] = (
        resid
        + gates[0] * branches[0]
        + gates[1] * branches[1]
        + keep * ffn_norm
        + (weight_one * one_vec) * vec_one
        + (weight_two * two_vec) * vec_two
    ).astype(BF16)
    dot_norm = jnp.sum(upstream * ffn_norm, axis=1, keepdims=True)
    dot_one = jnp.sum(upstream * vec_one, axis=1, keepdims=True)
    dot_two = jnp.sum(upstream * vec_two, axis=1, keepdims=True)
    grads = []
    for route, branch in zip(routes, branches):
        grads.append(
            jnp.sum(branch * upstream, axis=1, keepdims=True)
            + jnp.where(route == experts + 1, dot_norm, 0.0)
            + jnp.where(route == experts + 2, one_keep * dot_norm + one_vec * dot_one, 0.0)
            + jnp.where(route == experts + 3, two_keep * dot_norm + two_vec * dot_two, 0.0)
        )
    mean_grad = gates[0] * grads[0] + gates[1] * grads[1]
    lane = iota((BLOCK, LANES), 1)
    wide = jnp.zeros((BLOCK, LANES), F32)
    for route, gate, grad in zip(routes, gates, grads):
        wide = jnp.where(lane == route, gate * (grad - mean_grad), wide)
    for index, keep_part, vec_part, grad_weight, dot in (
        (kinds, one_keep, one_vec, weight_one, dot_one),
        (kinds + 2, two_keep, two_vec, weight_two, dot_two),
    ):
        keep_grad = grad_weight * dot_norm
        vec_grad = grad_weight * dot
        both = keep_part * keep_grad + vec_part * vec_grad
        wide = jnp.where(lane == index, keep_part * (keep_grad - both), wide)
        wide = jnp.where(lane == index + 1, vec_part * (vec_grad - both), wide)
    wide_low = wide.astype(BF16)
    wide_back = wide_low.astype(F32)
    minor_ref[...] += nn(wide_back.T.astype(BF16), low)
    share = jnp.where(lane == 0, weight_one * one_vec, 0.0)
    share = jnp.where(lane == 1, weight_two * two_vec, share)
    high, rest = split_low(share.T)
    vec_ref[...] += nn(high, cot) + nn(rest, cot)
    prev_ref[...] = nn(wide_low, mix_ref[...])[:, 0:kinds]
    gmix_ref[...] += jnp.dot(
        prevt_ref[...], wide_back, precision=HIGHEST_PRECISION, preferred_element_type=F32
    )
    grad_two = back + nt(wide_low, small_ref[...]) + keep * upstream
    gain_ref[...] += jnp.sum(grad_two * normed, axis=0, keepdims=True)
    mid = upstream + norm_back(grad_two * gain, normed, inverse)
    mid_ref[...] = mid
    proj = mid.astype(BF16)
    proj_ref[...] = proj
    attn = nt(proj, wo_ref[...]).astype(BF16)
    attn_ref[...] = attn
    high, rest = split_low(attn.astype(F32) * ao_ref[...].astype(F32))
    delta_ref[...] = nt(ind_ref[...], high) + nt(ind_ref[...], rest)


def attend_back_kernel(
    gain_row, qkv_ref, grad_ref, lse_ref, delta_ref, cos_ref, sin_ref, segc_ref, segr_ref,
    wq_ref, wk_ref, wv_ref, attn_in_ref, ao_ref, proj_ref, tok_ref, mid_ref, small_ref,
    weight_ref, gtok_ref, gain_ref, dq_ref, dk_ref, dv_ref, bias_ref, in_t_ref, ao_t_ref, acc_ref,
):
    step = pl.program_id(0)
    tokens = tok_ref.shape[0]
    blocks = tokens // BLOCK
    reach = DOC_MAX // BLOCK

    @pl.when(step == 0)
    def _():
        in_t_ref[...] = attn_in_ref[...].T
        ao_t_ref[...] = ao_ref[...].T
        acc_ref[...] = jnp.zeros_like(acc_ref)

    dq_ref[...] = jnp.zeros_like(dq_ref)
    for block in range(blocks):
        first = block * BLOCK
        last = min(blocks, block + reach + 1) * BLOCK
        span = last - first
        keys = slice(first, first + BLOCK)
        key_ids = iota((BLOCK, span), 0) + first
        row_ids = iota((BLOCK, span), 1) + first
        seen = (key_ids <= row_ids) & (segc_ref[keys, :] == segr_ref[0:1, first:last])
        bias_ref[:, 0:span] = jnp.where(seen, 0.0, NEGATIVE)
        key = qkv_ref[1, keys, :]
        value = qkv_ref[2, keys, :]
        key_grad = None
        for head in range(GROUP):
            mask = head_mask(head)
            index = step * GROUP + head
            query = qkv_ref[0, first:last, :] * mask
            upstream = grad_ref[first:last, :] * mask
            scores = nt(key, query) + bias_ref[:, 0:span]
            probs = jnp.exp(scores - lse_ref[pl.ds(index, 1), first:last])
            prob_grad = nt(value, upstream)
            score_grad = (probs * (prob_grad - delta_ref[pl.ds(index, 1), first:last])).astype(BF16)
            dv = nn(probs.astype(BF16), upstream)
            dk = nn(score_grad, query)
            dq_ref[first:last, :] += tn(score_grad, key * mask)
            key_grad = dk if key_grad is None else key_grad + dk
            value_grad = dv if head == 0 else value_grad + dv
        dk_ref[keys, :] = key_grad
        dv_ref[keys, :] = value_grad.astype(BF16)

    @pl.loop(0, blocks)
    def _(block):
        rows = pl.ds(pl.multiple_of(block * BLOCK, BLOCK), BLOCK)
        cosines = cos_ref[rows, :]
        sines = -sin_ref[rows, :]
        dq = turn(dq_ref[rows, :] * HEAD_DIM**-0.5, cosines, sines)
        dk = turn(dk_ref[rows, :], cosines, sines)
        dq_ref[rows, :] = dq
        dk_ref[rows, :] = dk
        acc_ref[rows, :] += (
            nt(dq.astype(BF16), wq_ref[...])
            + nt(dk.astype(BF16), wk_ref[...])
            + nt(dv_ref[rows, :], wv_ref[...])
        )

    halves = GROUP_LANES // LANES
    for index, (turned, grads) in enumerate(
        ((in_t_ref, dq_ref), (in_t_ref, dk_ref), (in_t_ref, dv_ref), (ao_t_ref, proj_ref))
    ):
        product = nn(turned[...], grads[...].astype(BF16)).astype(BF16)
        for half in range(halves):
            weight_ref[index * halves + half] = product[:, half * LANES : (half + 1) * LANES]

    @pl.when(step == pl.num_programs(0) - 1)
    def _():
        gain = small_ref[...].astype(F32).T[gain_row : gain_row + 1, :]
        gain_ref[...] = jnp.zeros_like(gain_ref)

        @pl.loop(0, blocks)
        def _(block):
            rows = pl.ds(pl.multiple_of(block * BLOCK, BLOCK), BLOCK)
            values = tok_ref[rows, :].astype(F32)
            inverse = inverse_rms(values)
            normed = values * inverse
            grad = acc_ref[rows, :]
            gain_ref[...] += jnp.sum(grad * normed, axis=0, keepdims=True)
            gtok_ref[rows, :] = mid_ref[rows, :] + norm_back(grad * gain, normed, inverse)


def add_low(left, right):
    return (left.astype(F32) + right.astype(F32)).astype(BF16)


def over_parts(values, bit):
    return lax.ppermute(values, "dp", [(d, d ^ bit) for d in range(8)])


def greet(targets):
    barrier = pltpu.get_barrier_semaphore()
    for present, target in targets:
        @pl.when(present)
        def _():
            pl.semaphore_signal(barrier, inc=1, device_id=target, device_id_type=MESH)
    pl.semaphore_wait(barrier, sum(present.astype(jnp.int32) for present, _ in targets))


def gather_kernel(
    part_ref, cot_ref, target_ref, out_ref, rows_ref, outgoing, send_sem, recv_sem, local_sem,
    row_send, row_recv, own_sem,
):
    me = lax.axis_index("dp")
    owner = lax.axis_index("expert")
    here, flank = me // 2, me % 2
    core = owner % 2
    up = ((2 * jnp.minimum(here + 1, 3) + flank), here < 3)
    down = ((2 * jnp.maximum(here - 1, 0) + flank), here > 0)
    across = 2 * here + 1 - flank
    partner = owner + 1 - 2 * core
    always = here >= 0
    routes = (
        (up[1], {"dp": up[0]}),
        (down[1], {"dp": down[0]}),
        (always, {"dp": across}),
        (always, {"expert": partner}),
    )
    side = owner // 2
    beside = owner + 2 - 4 * side
    corner = partner + 2 - 4 * side
    peers = (beside, corner, partner, owner)
    greet((*routes, (always, {"expert": beside}), (always, {"expert": corner})))

    def row_copy(slot):
        return pltpu.make_async_remote_copy(
            src_ref=outgoing.at[slot],
            dst_ref=rows_ref.at[owner],
            send_sem=row_send.at[slot],
            recv_sem=row_recv.at[slot],
            device_id={"expert": peers[slot]},
            device_id_type=MESH,
        )

    def copy(index, half, route, source=None):
        return pltpu.make_async_remote_copy(
            src_ref=out_ref.at[index, half] if source is None else source,
            dst_ref=out_ref.at[index, half],
            send_sem=send_sem.at[route, index],
            recv_sem=recv_sem.at[half, index],
            device_id=routes[route][1],
            device_id_type=MESH,
        )

    def arrive(index, half):
        copy(index, half, 2).wait_recv()

    local = pltpu.make_async_copy(part_ref, out_ref.at[me], local_sem)
    local.start()
    for route in range(3):
        @pl.when(routes[route][0])
        def _():
            copy(me, core, route, part_ref.at[core]).start()
    tokens = cot_ref.shape[0]
    for slot, peer in enumerate(peers):
        slots = iota((CAP, tokens), 0) + peer * CAP
        hot = (target_ref[0:1, :] == slots) | (target_ref[1:2, :] == slots)
        outgoing[slot] = nn(hot.astype(F32).astype(BF16), cot_ref[...]).astype(BF16)
        if slot > 0:
            row_copy(slot - 1).start()
    own_rows = pltpu.make_async_copy(outgoing.at[3], rows_ref.at[owner], own_sem)
    own_rows.start()
    for distance in range(1, 5):
        for toward, forward, present in (
            (here - distance, 0, here >= distance),
            (here + distance, 1, here + distance <= 3),
        ):
            index = 2 * jnp.clip(toward, 0, 3) + flank

            @pl.when(present)
            def _():
                arrive(index, core)
                copy(index, core, 2).start()
                copy(index, core, 3).start()

            @pl.when(present & routes[forward][0])
            def _():
                copy(index, core, forward).start()
        for sign in (-1, 1):
            if distance == 1 and sign == 1:
                continue
            toward = here + sign * (distance - 1)
            index = 2 * jnp.clip(toward, 0, 3) + 1 - flank

            @pl.when((toward >= 0) & (toward <= 3))
            def _():
                arrive(index, core)
                copy(index, core, 3).start()
    for offset in range(1, 8):
        index = (me + offset) % 8
        arrive(index, 1 - core)
        copy(index, core, 3).wait_send()
    local.wait()
    for route in range(3):
        @pl.when(routes[route][0])
        def _():
            copy(me, core, route, part_ref.at[core]).wait_send()
    for distance in range(1, 4):
        for toward, forward, present in (
            (here - distance, 0, here >= distance),
            (here + distance, 1, here + distance <= 3),
        ):
            index = 2 * jnp.clip(toward, 0, 3) + flank

            @pl.when(present)
            def _():
                copy(index, core, 2).wait_send()

            @pl.when(present & routes[forward][0])
            def _():
                copy(index, core, forward).wait_send()
    for slot in range(3):
        row_copy(slot).wait_recv()
        row_copy(slot).wait_send()
    own_rows.wait()


def gather_parts(packed, cotangent, target_row):
    rows, columns = packed.shape
    width = cotangent.shape[1]
    whole, cot_rows = pl.pallas_call(
        gather_kernel,
        in_specs=[pl.BlockSpec(memory_space=pltpu.VMEM)] * 3,
        out_specs=[pl.BlockSpec(memory_space=pl.ANY)] * 2,
        out_shape=[
            jax.ShapeDtypeStruct((8, 2, rows // 2, columns), BF16),
            jax.ShapeDtypeStruct((4, CAP, width), BF16),
        ],
        scratch_shapes=[
            pltpu.VMEM((4, CAP, width), BF16),
            pltpu.SemaphoreType.DMA((4, 8)),
            pltpu.SemaphoreType.DMA((2, 8)),
            pltpu.SemaphoreType.DMA,
            pltpu.SemaphoreType.DMA((3,)),
            pltpu.SemaphoreType.DMA((3,)),
            pltpu.SemaphoreType.DMA,
        ],
        compiler_params=params(collective_id=0, has_side_effects=True),
        cost_estimate=cost(10e9, 10e6),
        name="gather_parts",
    )(packed.reshape(2, rows // 2, columns), cotangent, target_row)
    return whole.reshape(8 * rows, columns), cot_rows


def add_planes(target, left, right):
    @pl.loop(0, target.shape[0])
    def _(index):
        total = left[index].astype(F32) + right[index].astype(F32)
        target[index] = total.astype(target.dtype)


def reduce_kernel(
    gate_ref, up_ref, risen_ref, fallen_ref, pair_ref, weight_ref, minor_ref,
    gate_out, up_out, down_out, weight_out, minor_out,
    gate_in, up_in, line_in, gate_stage, up_stage, line_stage, pair_in, core_in, core_sum, side_in, side_sum, cross_in, line_ref, line_sum_ref,
    small_in, small_sum, piece_send, piece_recv, other_send, other_recv,
):
    me = lax.axis_index("dp")
    owner = lax.axis_index("expert")
    here, flank = me // 2, me % 2
    core, side = owner % 2, owner // 2
    rising = {"dp": 2 * jnp.minimum(here + 1, 3) + flank}
    falling = {"dp": 2 * jnp.maximum(here - 1, 0) + flank}
    across = {"dp": me + 1 - 2 * flank}
    partner = {"expert": owner + 1 - 2 * core}
    beside = {"expert": owner + 2 - 4 * side}
    always = here >= 0
    greet(((here < 3, rising), (here > 0, falling), (always, across), (always, partner),
           (always, beside)))
    pieces = (
        (gate_ref, gate_in, gate_stage),
        (up_ref, up_in, up_stage),
        (line_ref, line_in, line_stage),
    )

    def piece_copy(piece, turn_index, way, source):
        return pltpu.make_async_remote_copy(
            src_ref=source,
            dst_ref=pieces[piece][1].at[way, turn_index],
            send_sem=piece_send.at[piece, turn_index, way],
            recv_sem=piece_recv.at[piece, turn_index, way],
            device_id=(rising, falling)[way],
            device_id_type=MESH,
        )

    def other_copy(index, source, target, device):
        return pltpu.make_async_remote_copy(
            src_ref=source, dst_ref=target, send_sem=other_send.at[index],
            recv_sem=other_recv.at[index], device_id=device, device_id_type=MESH,
        )

    def direct(piece, turn_index):
        own = pieces[piece][0]

        @pl.when(here == 0)
        def _():
            piece_copy(piece, turn_index, 0, own.at[3 - turn_index]).start()

        @pl.when(here == 3)
        def _():
            piece_copy(piece, turn_index, 1, own.at[turn_index]).start()

    def relayed(turn_index):
        return (
            (0, (here > 0) & (here < 3 - turn_index), 3 - turn_index),
            (1, (here < 3) & (here > turn_index), turn_index),
        )

    def relay(piece, turn_index):
        own, landed, stage = pieces[piece]
        for way, present, chunk in relayed(turn_index):
            if piece == 0:
                present = present & ((here != 1) if way == 0 else (here != 2))

            @pl.when(present)
            def _():
                copy = piece_copy(piece, turn_index, way, stage.at[way, turn_index])
                copy.wait_recv()
                add_planes(
                    stage.at[way, turn_index], own.at[chunk], landed.at[way, turn_index]
                )
                copy.start()

    def early(turn_index):
        own, landed, stage = pieces[0]
        for way, place, chunk in ((0, 1, 3 - turn_index), (1, 2, turn_index)):
            @pl.when(here == place)
            def _():
                add_planes(
                    stage.at[way, turn_index], own.at[chunk], landed.at[way, turn_index]
                )
                piece_copy(0, turn_index, way, stage.at[way, turn_index]).start()

    def finish(piece, target):
        own, landed, stage = pieces[piece]
        lower = jnp.minimum(3 - here, 2)
        upper = jnp.minimum(here, 2)

        @pl.when((here > (1 if piece == 0 else 0)))
        def _():
            piece_copy(piece, lower, 0, stage.at[0, 0]).wait_recv()

        @pl.when(here < (2 if piece == 0 else 3))
        def _():
            piece_copy(piece, upper, 1, stage.at[0, 0]).wait_recv()

        @pl.when(here == 0)
        def _():
            add_planes(target, own.at[here], landed.at[1, upper])

        @pl.when(here == 3)
        def _():
            add_planes(target, own.at[here], landed.at[0, lower])

        @pl.when((here > 0) & (here < 3))
        def _():
            @pl.loop(0, target.shape[0])
            def _(index):
                total = (
                    own[here, index].astype(F32)
                    + landed[0, lower, index].astype(F32)
                    + landed[1, upper, index].astype(F32)
                )
                target[index] = total.astype(target.dtype)

    def drain(piece):
        own, _, stage = pieces[piece]
        for turn_index in range(0 if piece == 0 else 3):
            @pl.when(here == 0)
            def _():
                piece_copy(piece, turn_index, 0, own.at[3 - turn_index]).wait_send()

            @pl.when(here == 3)
            def _():
                piece_copy(piece, turn_index, 1, own.at[turn_index]).wait_send()
        for turn_index in range(2):
            for way, present, _ in relayed(turn_index):
                @pl.when(present)
                def _():
                    piece_copy(
                        piece, turn_index, way, stage.at[way, turn_index]
                    ).wait_send()

    half = core_in.shape[0]
    quarter = half // 2
    core_weight = other_copy(0, weight_ref.at[pl.ds(half * (1 - core), half)], core_in, partner)
    core_small = other_copy(1, minor_ref, small_in.at[0], partner)
    side_weight = other_copy(2, core_sum.at[pl.ds(quarter * (1 - side), quarter)], side_in, beside)
    side_small = other_copy(3, small_sum.at[0], small_in.at[1], beside)
    cross_weight = [
        other_copy(4 + z, side_sum.at[:, 2 * z + 1 - flank], cross_in.at[z], across)
        for z in range(4)
    ]
    cross_small = other_copy(8, small_sum.at[1], small_in.at[2], across)
    rise_small = other_copy(9, small_sum.at[3], small_in.at[3], rising)
    fall_small = other_copy(10, small_sum.at[4], small_in.at[4], falling)
    mine = half * core + quarter * side
    own_part = weight_out.at[pl.ds(mine, quarter)]
    own_half = weight_out.at[pl.ds(half * core, half)]
    side_back = other_copy(11, own_part, own_part, beside)
    core_back = other_copy(12, own_half, own_half, partner)

    pair_copy = other_copy(13, pair_ref.at[1 - flank], pair_in, across)
    core_weight.start()
    core_small.start()
    pair_copy.start()
    for turn_index in range(3):
        direct(1, turn_index)

    @pl.when(here == 1)
    def _():
        for turn_index in range(3):
            gate_in[0, turn_index] = risen_ref[2 - turn_index]

    @pl.when(here == 2)
    def _():
        for turn_index in range(3):
            gate_in[1, turn_index] = fallen_ref[turn_index]

    for turn_index in range(2):
        early(turn_index)
    core_weight.wait_recv()
    core_small.wait_recv()
    add_planes(core_sum, weight_ref.at[pl.ds(half * core, half)], core_in)
    small_sum[0] = minor_ref[...] + small_in[0]
    side_weight.start()
    side_small.start()
    for piece in (0, 1):
        relay(piece, 0)
    pair_copy.wait_recv()
    add_planes(down_out, pair_ref.at[flank], pair_in)
    side_weight.wait_recv()
    side_small.wait_recv()
    add_planes(side_sum, core_sum.at[pl.ds(quarter * side, quarter)], side_in)
    small_sum[1] = small_sum[0] + small_in[1]
    for copy in cross_weight:
        copy.start()
    cross_small.start()
    for piece in (0, 1):
        relay(piece, 1)
    for copy in cross_weight:
        copy.wait_recv()
    cross_small.wait_recv()
    for z in range(4):
        add_planes(line_ref.at[z], side_sum.at[:, 2 * z + flank], cross_in.at[z])
    small_sum[2] = small_sum[1] + small_in[2]
    small_sum[3] = small_sum[2]
    small_sum[4] = small_sum[2]
    for turn_index in range(3):
        direct(2, turn_index)

    @pl.when(here == 0)
    def _():
        rise_small.start()

    @pl.when(here == 3)
    def _():
        fall_small.start()

    for turn_index in range(2):
        relay(2, turn_index)

    @pl.when(here > 0)
    def _():
        rise_small.wait_recv()
        small_sum[3] = small_sum[2] + small_in[3]

    @pl.when((here > 0) & (here < 3))
    def _():
        rise_small.start()

    @pl.when(here < 3)
    def _():
        fall_small.wait_recv()
        small_sum[4] = small_sum[2] + small_in[4]

    @pl.when((here > 0) & (here < 3))
    def _():
        fall_small.start()

    minor_out[...] = small_sum[3] + small_sum[4] - small_sum[2]
    finish(2, line_sum_ref)
    for index in range(quarter):
        weight_out[mine + index] = line_sum_ref[index]
    side_back.start()
    finish(0, gate_out)
    side_back.wait_recv()
    core_back.start()
    finish(1, up_out)
    core_back.wait_recv()
    for piece in range(3):
        drain(piece)
    for copy in (core_weight, core_small, side_weight, side_small, *cross_weight, cross_small,
                 side_back, core_back, pair_copy):
        copy.wait_send()

    @pl.when(here < 3)
    def _():
        rise_small.wait_send()

    @pl.when(here > 0)
    def _():
        fall_small.wait_send()


def reduce_parts(kept, down, weights, minor):
    gate, up = kept[:2]
    kept = [piece.reshape(-1, piece.shape[1] // 32, 32, piece.shape[2]) for piece in kept]
    pair = down.reshape(2, down.shape[1] // 32, 32, down.shape[2])
    blocks, width, lanes = weights.shape
    rows = width // 8
    plane = (rows, lanes)
    chunks = [piece.shape[1:] for piece in kept[:2]]
    line = (blocks // 4,) + plane
    low = [pltpu.VMEM((2, 3) + chunk, BF16) for chunk in chunks + [line]]
    stages = [pltpu.VMEM((2, 2) + chunk, BF16) for chunk in chunks + [line]]
    outs = pl.pallas_call(
        reduce_kernel,
        in_specs=[pl.BlockSpec(memory_space=pltpu.VMEM)] * 7,
        out_specs=[pl.BlockSpec(memory_space=pltpu.VMEM)] * 5,
        out_shape=[jax.ShapeDtypeStruct(chunk, F32) for chunk in chunks + [pair.shape[1:]]]
        + [
            jax.ShapeDtypeStruct((blocks,) + plane, BF16),
            jax.ShapeDtypeStruct(minor.shape, F32),
        ],
        scratch_shapes=[
            *low,
            *stages,
            pltpu.VMEM(pair.shape[1:], BF16),
            pltpu.VMEM((blocks // 2, 8) + plane, BF16),
            pltpu.VMEM((blocks // 2, 8) + plane, BF16),
            pltpu.VMEM((blocks // 4, 8) + plane, BF16),
            pltpu.VMEM((blocks // 4, 8) + plane, BF16),
            pltpu.VMEM((4,) + line, BF16),
            pltpu.VMEM((4,) + line, BF16),
            pltpu.VMEM(line, BF16),
            pltpu.VMEM((5,) + minor.shape, F32),
            pltpu.VMEM((5,) + minor.shape, F32),
            pltpu.SemaphoreType.DMA((3, 3, 2)),
            pltpu.SemaphoreType.DMA((3, 3, 2)),
            pltpu.SemaphoreType.DMA((14,)),
            pltpu.SemaphoreType.DMA((14,)),
        ],
        compiler_params=params(collective_id=1, has_side_effects=True),
        name="reduce_parts",
    )(*kept, pair, weights.reshape(blocks, 8, rows, lanes), minor)
    shapes = (gate.shape[1:], up.shape[1:], down.shape[1:])
    shares = [out.reshape(shape) for out, shape in zip(outs, shapes)]
    return shares, outs[3], outs[4]


FF_TILE = 256


def exchange_kernel(
    send_ref, cot_ref, win_ref, wout_ref,
    gate_keep, gate_away, up_keep, up_away, own_down, one_down, two_down, three_down, return_out,
    recv, cot, gate_w, up_w, down_w, front, turned, out_acc, row_acc, ret, gate_g, up_g, down_g,
    token_send, token_recv, back_send, back_recv, load_sem, weight_sem, store_sem, down_sem, own_sem,
):
    me = lax.axis_index("expert")
    spot = lax.axis_index("dp")
    here, flank = spot // 2, spot % 2
    line_peers = (here, here + 1 - 2 * (here % 2), here + 2 - 4 * (here // 2), 3 - here)
    down_parts = (own_down, one_down, two_down, three_down)
    share = gate_w.shape[0] // 8
    core, side = me % 2, me // 2
    partner = me + 1 - 2 * core
    beside = me + 2 - 4 * side
    corner = partner + 2 - 4 * side
    peers = (me, beside, corner, partner)
    always = me >= 0
    width = out_acc.shape[1]
    ff = down_w.shape[0]
    tiles = ff // FF_TILE
    greet([(always, {"expert": peer}) for peer in peers[1:]])

    def token_copy(slot):
        return pltpu.make_async_remote_copy(
            src_ref=send_ref.at[peers[slot]], dst_ref=recv.at[slot],
            send_sem=token_send.at[slot], recv_sem=token_recv.at[slot],
            device_id={"expert": peers[slot]}, device_id_type=MESH,
        )

    def back_copy(slot):
        return pltpu.make_async_remote_copy(
            src_ref=ret.at[slot], dst_ref=return_out.at[me],
            send_sem=back_send.at[slot], recv_sem=back_recv.at[slot],
            device_id={"expert": peers[slot]}, device_id_type=MESH,
        )

    def tile_slice(tile):
        return pl.ds(pl.multiple_of(tile * FF_TILE, FF_TILE), FF_TILE)

    def weight_copies(tile):
        cols = tile_slice(tile)
        shifted = pl.ds(pl.multiple_of(ff + tile * FF_TILE, FF_TILE), FF_TILE)
        return (
            pltpu.make_async_copy(
                win_ref.at[:, cols], gate_w.at[:, cols], weight_sem.at[0, tile]
            ),
            pltpu.make_async_copy(
                win_ref.at[:, shifted], up_w.at[:, cols], weight_sem.at[1, tile]
            ),
            pltpu.make_async_copy(
                wout_ref.at[cols, :], down_w.at[cols, :], weight_sem.at[2, tile]
            ),
        )

    def side_copy(piece, index, kept):
        source = (gate_g, up_g)[piece].at[index * share : (index + 1) * share, :]
        target = ((gate_away, gate_keep), (up_away, up_keep))[piece][kept].at[index // 2]
        return pltpu.make_async_copy(source, target, store_sem.at[piece, index])

    def down_copy(tile, distance):
        return pltpu.make_async_copy(
            down_g.at[tile_slice(tile), :], down_parts[distance].at[tile % 2], down_sem.at[tile]
        )

    for slot in (1, 2, 3):
        token_copy(slot).start()
    loads = [pltpu.make_async_copy(send_ref.at[me], recv.at[0], load_sem.at[0])] + [
        pltpu.make_async_copy(cot_ref.at[peers[slot]], cot.at[slot], load_sem.at[1 + slot])
        for slot in range(4)
    ]
    for load in loads:
        load.start()

    @pl.loop(0, tiles)
    def _(tile):
        for copy in weight_copies(tile):
            copy.start()

    for load in loads:
        load.wait()

    def work(slot):
        extra = recv[slot, :, width:].astype(F32)
        gate_weight = extra[:, 0:1] + extra[:, 1:2]
        out_acc[...] = jnp.zeros_like(out_acc)
        row_acc[...] = jnp.zeros_like(row_acc)

        @pl.loop(0, tiles)
        def _(tile):
            cols = tile_slice(tile)
            if slot == 0:
                for copy in weight_copies(tile):
                    copy.wait()
            token = recv[slot, :, 0:width]
            gate = nn(token, gate_w[:, cols])
            up = nn(token, up_w[:, cols])
            grad = nt(cot[slot], down_w[cols, :]) * gate_weight
            sig = jax.nn.sigmoid(gate)
            act = gate * sig
            hidden = act * up
            out_acc[...] += nn(hidden.astype(BF16), down_w[cols, :])
            front[2, slot, :, cols] = (hidden * gate_weight).astype(BF16)
            gate_grad = (grad * up * sig * (1.0 + gate * (1.0 - sig))).astype(BF16)
            up_grad = (grad * act).astype(BF16)
            front[0, slot, :, cols] = gate_grad
            front[1, slot, :, cols] = up_grad
            row_acc[...] += nt(gate_grad, gate_w[:, cols]) + nt(up_grad, up_w[:, cols])

        ret[slot, 0:CAP, :] = out_acc[...].astype(BF16)
        ret[slot, CAP:, :] = row_acc[...].astype(BF16)
        turned[:, slot * CAP : (slot + 1) * CAP] = recv[slot, :, 0:width].T

    own_back = pltpu.make_async_copy(ret.at[0], return_out.at[me], own_sem)
    work(0)
    own_back.start()
    for slot in (1, 2, 3):
        token_copy(slot).wait_recv()
        work(slot)
        back_copy(slot).start()
    total = 4 * CAP

    @pl.loop(0, tiles)
    def _(tile):
        cols = tile_slice(tile)
        hidden = front[2, :, :, cols].reshape(total, FF_TILE)
        down_g[cols, :] = tn(hidden, cot[...].reshape(total, width)).astype(BF16)
        gate_g[:, cols] = nn(turned[...], front[0, :, :, cols].reshape(total, FF_TILE)).astype(BF16)
        up_g[:, cols] = nn(turned[...], front[1, :, :, cols].reshape(total, FF_TILE)).astype(BF16)
        for distance in range(4):
            @pl.when(tile // 2 == line_peers[distance])
            def _():
                down_copy(tile, distance).start()

    for piece in range(2):
        for index in range(8):
            for kept in range(2):
                @pl.when((flank == index % 2) if kept else (flank != index % 2))
                def _():
                    side_copy(piece, index, kept).start()

    for slot in (1, 2, 3):
        token_copy(slot).wait_send()
        back_copy(slot).wait_recv()
        back_copy(slot).wait_send()
    own_back.wait()

    for piece in range(2):
        for index in range(8):
            side_copy(piece, index, 1).wait()

    @pl.loop(0, tiles)
    def _(tile):
        down_copy(tile, 0).wait()


def exchange_experts(send, cot_rows, w_in, w_out):
    peers, cap, payload = send.shape
    ff, width = w_out.shape
    anywhere = pl.BlockSpec(memory_space=pl.ANY)
    tiles = ff // FF_TILE
    *grads, returned = pl.pallas_call(
        exchange_kernel,
        in_specs=[anywhere] * 4,
        out_specs=[anywhere] * 9,
        out_shape=[jax.ShapeDtypeStruct((4, width // 8, ff), BF16)] * 4
        + [jax.ShapeDtypeStruct((2, ff // 8, width), BF16)] * 4
        + [jax.ShapeDtypeStruct((peers, 2 * cap, width), BF16)],
        scratch_shapes=[
            pltpu.VMEM((peers, cap, payload), BF16),
            pltpu.VMEM((peers, cap, width), BF16),
            pltpu.VMEM((width, ff), BF16),
            pltpu.VMEM((width, ff), BF16),
            pltpu.VMEM((ff, width), BF16),
            pltpu.VMEM((3, peers, cap, ff), BF16),
            pltpu.VMEM((width, peers * cap), BF16),
            pltpu.VMEM((cap, width), F32),
            pltpu.VMEM((cap, width), F32),
            pltpu.VMEM((peers, 2 * cap, width), BF16),
            pltpu.VMEM((width, ff), BF16),
            pltpu.VMEM((width, ff), BF16),
            pltpu.VMEM((ff, width), BF16),
            pltpu.SemaphoreType.DMA((4,)),
            pltpu.SemaphoreType.DMA((4,)),
            pltpu.SemaphoreType.DMA((4,)),
            pltpu.SemaphoreType.DMA((4,)),
            pltpu.SemaphoreType.DMA((5,)),
            pltpu.SemaphoreType.DMA((3, tiles)),
            pltpu.SemaphoreType.DMA((2, 8)),
            pltpu.SemaphoreType.DMA((tiles,)),
            pltpu.SemaphoreType.DMA,
        ],
        compiler_params=params(collective_id=2, has_side_effects=True),
        cost_estimate=cost(18 * peers * cap * width * ff, 40e6),
        name="exchange_experts",
    )(send, cot_rows.reshape(peers, cap, width), w_in, w_out)
    return grads, returned


def plain_experts(send, cot_rows, w_in_one, w_out_one, swap):
    experts, _, payload = send.shape
    ff, width = w_out_one.shape
    recv = swap(send).reshape(experts * CAP, payload)

    slot_count = experts * CAP
    ff_tile = 256
    ff_tiles = ff // ff_tile
    slot_full = whole_block((slot_count, width))
    recv_full = whole_block((slot_count, payload))
    front_spec = pl.BlockSpec((3, slot_count, ff_tile), lambda j: (0, 0, j))
    front, ret = pl.pallas_call(
        expert_kernel,
        grid=(ff_tiles,),
        in_specs=[
            recv_full,
            slot_full,
            pl.BlockSpec((width, ff_tile), lambda j: (0, j)),
            pl.BlockSpec((width, ff_tile), lambda j: (0, ff_tiles + j)),
            pl.BlockSpec((ff_tile, width), lambda j: (j, 0)),
        ],
        out_specs=[front_spec, whole_block((experts, 2 * CAP, width))],
        out_shape=[
            jax.ShapeDtypeStruct((3, slot_count, ff), BF16),
            jax.ShapeDtypeStruct((experts, 2 * CAP, width), BF16),
        ],
        scratch_shapes=[pltpu.VMEM((slot_count, width), F32)] * 2,
        compiler_params=params(),
        cost_estimate=cost(12 * slot_count * width * ff, 26e6),
        name="expert",
    )(recv, cot_rows, w_in_one, w_in_one, w_out_one)
    returned = swap(ret)
    expert_grads = pl.pallas_call(
        expert_grad_kernel,
        grid=(ff_tiles,),
        in_specs=[recv_full, slot_full, front_spec],
        out_specs=[
            pl.BlockSpec((width, ff_tile), lambda j: (0, j)),
            pl.BlockSpec((width, ff_tile), lambda j: (0, j)),
            pl.BlockSpec((ff_tile, width), lambda j: (j, 0)),
        ],
        out_shape=[
            jax.ShapeDtypeStruct((width, ff), BF16),
            jax.ShapeDtypeStruct((width, ff), BF16),
            jax.ShapeDtypeStruct((ff, width), BF16),
        ],
        scratch_shapes=[pltpu.VMEM((width, slot_count), BF16)],
        compiler_params=params(),
        cost_estimate=cost(6 * slot_count * width * ff, 24e6),
        name="expert_grad",
    )(recv, cot_rows, front)
    return expert_grads, returned


def per_device(
    tokens, prev_scores, segments, routes, wqkv, wo, router, const_gate, const_vec, gain1, gain2,
    gate_mix, w_in, w_out, cotangent,
):
    tok_count, width = tokens.shape
    kinds = router.shape[1]
    experts = w_in.shape[0] * lax.axis_size("expert")
    ff = w_out.shape[1]
    qkv_cols = wqkv.shape[1]
    parts = lax.axis_size("dp")
    by_hand = parts == 8 and experts == 4
    small = jnp.concatenate(
        [router, const_gate, const_vec, gain1[:, None], gain2[:, None]], axis=1
    )
    packed = jnp.concatenate(
        [wqkv, wo, jnp.pad(small, ((0, 0), (0, LANES - small.shape[1])))], axis=1
    )

    seq_len = segments.shape[1]
    positions = (jnp.arange(tok_count, dtype=jnp.int32) % seq_len).astype(F32)
    half = HEAD_DIM // 2
    frequency = 10000.0 ** (-jnp.arange(half).astype(F32) / half)
    angles = positions[:, None] * frequency[None, :]
    cosines = jnp.tile(jnp.cos(angles), (1, LANES // half))
    sines = jnp.tile(jnp.sin(angles), (1, LANES // half))
    signs = jnp.where(jnp.arange(LANES) % HEAD_DIM < half, -1.0, 1.0).astype(F32)
    sines = sines * signs[None, :]
    seg_col = segments.reshape(tok_count, 1)
    seg_row = segments.reshape(1, tok_count)

    names = jnp.arange(kinds, dtype=jnp.int32)
    hot = [routes[:, i : i + 1] == names[None, :] for i in range(2)]
    named = (hot[0] | hot[1]).astype(BF16)
    ids = jnp.arange(tok_count, dtype=jnp.int32)
    before = (ids[:, None] > ids[None, :]).astype(BF16)
    earlier = jnp.dot(before, named, preferred_element_type=F32)
    slots = [jnp.sum(jnp.where(h, earlier, 0.0), axis=1).astype(jnp.int32) for h in hot]
    targets = [
        jnp.where(routes[:, i] < experts, routes[:, i] * CAP + slots[i], experts * CAP)
        for i in range(2)
    ]
    target_row = jnp.stack(targets, axis=0)
    target_col = jnp.stack(targets, axis=1)
    prev_mix = jnp.dot(prev_scores, gate_mix.astype(F32), precision=HIGHEST_PRECISION)
    prev_mix = jnp.pad(prev_mix, ((0, 0), (0, LANES - kinds)))

    def swap(values):
        return lax.all_to_all(values, "expert", split_axis=0, concat_axis=0, tiled=True)

    if by_hand:
        whole, cot_rows = gather_parts(packed, cotangent, target_row)
    else:
        whole = lax.all_gather(packed, "dp", axis=0, tiled=True)
        cot_send = pl.pallas_call(
            functools.partial(send_cotangent_kernel, experts),
            out_shape=jax.ShapeDtypeStruct((experts, CAP, width), BF16),
            compiler_params=params(),
            cost_estimate=cost(2 * experts * CAP * tok_count * width, 4 * tok_count * width),
            name="send_cotangent",
        )(cotangent, target_row)
        cot_rows = swap(cot_send)
    cot_rows = cot_rows.reshape(experts * CAP, width)

    groups = HEADS // GROUP
    tiles = qkv_cols // 3 // GROUP_LANES
    weight_specs = [
        pl.BlockSpec((width, GROUP_LANES), functools.partial(lambda o, i: (0, o + i), part * tiles))
        for part in range(3)
    ]
    small_spec = pl.BlockSpec((width, LANES), lambda *_: (0, (qkv_cols + width) // LANES))
    wo_spec = pl.BlockSpec((width, width), lambda *_: (0, qkv_cols // width))
    table = whole_block((tok_count, LANES))
    full = whole_block((tok_count, width))
    group_spec = pl.BlockSpec((tok_count, GROUP_LANES), lambda i: (0, i))
    qkv_spec = pl.BlockSpec((3, tok_count, GROUP_LANES), lambda i: (0, 0, i))
    seg_specs = [whole_block((tok_count, 1)), whole_block((1, tok_count))]
    span = DOC_MAX + BLOCK
    head_rows = 16
    lse_spec = whole_block((head_rows, tok_count))
    qkv, attn_in, attn_out, lse = pl.pallas_call(
        functools.partial(attend_kernel, kinds + 6),
        grid=(groups,),
        in_specs=[full, *weight_specs, small_spec, table, table, *seg_specs],
        out_specs=[qkv_spec, full, group_spec, lse_spec],
        out_shape=[
            jax.ShapeDtypeStruct((3, tok_count, width), BF16),
            jax.ShapeDtypeStruct((tok_count, width), BF16),
            jax.ShapeDtypeStruct((tok_count, width), BF16),
            jax.ShapeDtypeStruct((head_rows, tok_count), F32),
        ],
        scratch_shapes=[
            pltpu.VMEM((1, width), F32),
            pltpu.VMEM((BLOCK, span), F32),
            pltpu.VMEM((tok_count, LANES), F32),
        ],
        compiler_params=params(),
        cost_estimate=cost(12e9, 16e6),
        name="attend",
    )(tokens, whole, whole, whole, whole, cosines, sines, seg_col, seg_row)

    payload = width + LANES
    resid_mid, scal, send = pl.pallas_call(
        functools.partial(middle_kernel, kinds),
        grid=(1,),
        in_specs=[
            full, wo_spec, full, small_spec, table, whole_block((tok_count, 2)),
            whole_block((2, tok_count)),
        ],
        out_specs=[full, table, whole_block((experts, CAP, payload))],
        out_shape=[
            jax.ShapeDtypeStruct((tok_count, width), F32),
            jax.ShapeDtypeStruct((tok_count, LANES), F32),
            jax.ShapeDtypeStruct((experts, CAP, payload), BF16),
        ],
        scratch_shapes=[
            pltpu.VMEM((tok_count, width), BF16),
            pltpu.VMEM((tok_count, LANES), BF16),
            pltpu.VMEM((tok_count, LANES), BF16),
        ],
        compiler_params=params(),
        cost_estimate=cost(3.5e9, 10e6),
        name="middle",
    )(attn_out, whole, tokens, whole, prev_mix, routes, target_row)
    w_in_one = w_in.reshape(width, 2 * ff)
    w_out_one = w_out.reshape(ff, width)
    if by_hand:
        expert_grads, returned = exchange_experts(send, cot_rows, w_in_one, w_out_one)
    else:
        expert_grads, returned = plain_experts(send, cot_rows, w_in_one, w_out_one, swap)
    returned, *expert_grads = lax.optimization_barrier((returned, *expert_grads))
    if by_hand:
        gate_keep, gate_away, up_keep, up_away, *down_parts = expert_grads
        gate_pair = (gate_keep, over_parts(gate_away, 1))
        up_pair = (up_keep, over_parts(up_away, 1))
        lined = [down_parts[0]]
        for i in (1, 2, 3):
            lined.append(over_parts(down_parts[i], 2 * i))

    mix_turned = jnp.pad(gate_mix.T, ((0, LANES - kinds), (0, LANES - kinds)))
    indicator = (
        jnp.arange(width)[None, :] // HEAD_DIM == jnp.arange(head_rows)[:, None]
    ).astype(BF16)
    token_block = pl.BlockSpec((BLOCK, width), lambda i: (i, 0))
    table_block = pl.BlockSpec((BLOCK, LANES), lambda i: (i, 0))
    two_block = pl.BlockSpec((BLOCK, 2), lambda i: (i, 0))
    (
        mixed, grad_prev, mid_grad, proj_grad, attn_grad, delta, minor, vec, gain2_row, grad_mix,
    ) = pl.pallas_call(
        functools.partial(combine_kernel, kinds, experts),
        grid=(tok_count // BLOCK,),
        in_specs=[
            whole_block((experts, 2 * CAP, width)), two_block, two_block, table_block,
            token_block, token_block, token_block, small_spec, wo_spec,
            whole_block((LANES, LANES)),
            pl.BlockSpec((kinds, BLOCK), lambda i: (0, i)),
            whole_block((head_rows, width)),
        ],
        out_specs=[
            token_block, pl.BlockSpec((BLOCK, kinds), lambda i: (i, 0)), token_block, token_block,
            token_block, pl.BlockSpec((head_rows, BLOCK), lambda i: (0, i)),
            whole_block((LANES, width)), whole_block((LANES, width)), whole_block((1, width)),
            whole_block((kinds, LANES)),
        ],
        out_shape=[
            jax.ShapeDtypeStruct((tok_count, width), BF16),
            jax.ShapeDtypeStruct((tok_count, kinds), F32),
            jax.ShapeDtypeStruct((tok_count, width), F32),
            jax.ShapeDtypeStruct((tok_count, width), BF16),
            jax.ShapeDtypeStruct((tok_count, width), BF16),
            jax.ShapeDtypeStruct((head_rows, tok_count), F32),
            jax.ShapeDtypeStruct((LANES, width), F32),
            jax.ShapeDtypeStruct((LANES, width), F32),
            jax.ShapeDtypeStruct((1, width), F32),
            jax.ShapeDtypeStruct((kinds, LANES), F32),
        ],
        scratch_shapes=[pltpu.VMEM((LANES, width), F32)],
        compiler_params=params(),
        cost_estimate=cost(1e6, 1e5),
        name="combine",
    )(
        returned, target_col, routes, scal, resid_mid, cotangent, attn_out, whole, whole,
        mix_turned, prev_scores.T, indicator,
    )

    if by_hand:
        gate_pair, attn_grad = lax.optimization_barrier((gate_pair, attn_grad))
        gate_met = add_low(*gate_pair)
        risen = lax.ppermute(gate_met[1:], "dp", [(0, 2), (1, 3)])
        fallen = lax.ppermute(gate_met[:3], "dp", [(6, 4), (7, 5)])
    halves = GROUP_LANES // LANES
    weights, grad_tokens, gain1_row = pl.pallas_call(
        functools.partial(attend_back_kernel, kinds + 6),
        grid=(groups,),
        in_specs=[
            qkv_spec, group_spec, lse_spec, lse_spec, table, table, *seg_specs, *weight_specs,
            full, full, group_spec, full, full, small_spec,
        ],
        out_specs=[
            pl.BlockSpec((4 * halves, width, LANES), lambda i: (i, 0, 0)), full,
            whole_block((1, width)),
        ],
        out_shape=[
            jax.ShapeDtypeStruct((4 * halves * groups, width, LANES), BF16),
            jax.ShapeDtypeStruct((tok_count, width), F32),
            jax.ShapeDtypeStruct((1, width), F32),
        ],
        scratch_shapes=[
            pltpu.VMEM((tok_count, GROUP_LANES), F32),
            pltpu.VMEM((tok_count, GROUP_LANES), F32),
            pltpu.VMEM((tok_count, GROUP_LANES), BF16),
            pltpu.VMEM((BLOCK, span), F32),
            pltpu.VMEM((width, tok_count), BF16),
            pltpu.VMEM((width, tok_count), BF16),
            pltpu.VMEM((tok_count, width), F32),
        ],
        compiler_params=params(),
        cost_estimate=cost(1e6, 1e5),
        name="attend_back",
    )(
        qkv, attn_grad, lse, delta, cosines, sines, seg_col, seg_row, whole, whole, whole,
        attn_in, attn_out, proj_grad, tokens, mid_grad, whole,
    )

    minor_rows = jnp.concatenate([minor[: kinds + 4], vec[:2], gain1_row, gain2_row], axis=0)
    minor_all = jnp.concatenate(
        [minor_rows, jnp.pad(grad_mix[:, :kinds], ((0, 0), (0, width - kinds)))], axis=0
    )
    rows = width // parts
    if by_hand:
        up_pair, lined, risen, fallen, weights = lax.optimization_barrier(
            (up_pair, lined, risen, fallen, weights)
        )
        kept = [gate_met, add_low(*up_pair), risen, fallen]
        shares, weight_sum, minor_all = reduce_parts(
            kept, sum(part.astype(F32) for part in lined).astype(BF16), weights, minor_all
        )
    else:
        shares = [
            lax.psum_scatter(grad, "dp", scatter_dimension=0, tiled=True).astype(F32)
            for grad in expert_grads
        ]
        weight_part = lax.psum_scatter(weights, "expert", scatter_dimension=0, tiled=True)
        weight_part = lax.psum_scatter(weight_part, "dp", scatter_dimension=1, tiled=True)
        weight_sum = lax.all_gather(weight_part, "expert", axis=0, tiled=True)
        minor_all = lax.psum(minor_all, ("dp", "expert"))
    grad_gate_mix = minor_all[kinds + 8 :, :kinds]
    minor_sum = lax.dynamic_slice_in_dim(
        minor_all[: kinds + 8], lax.axis_index("dp") * rows, rows, 1
    ).T
    weight_sum = weight_sum.reshape(groups, 4, -1, rows, LANES)
    weight_sum = weight_sum.transpose(3, 1, 0, 2, 4).reshape(rows, 4 * width).astype(F32)
    return (
        mixed,
        grad_tokens,
        grad_prev,
        weight_sum[:, :qkv_cols],
        weight_sum[:, qkv_cols:],
        minor_sum[:, :kinds],
        minor_sum[:, kinds : kinds + 4],
        minor_sum[:, kinds + 4 : kinds + 6],
        minor_sum[:, kinds + 6],
        minor_sum[:, kinds + 7],
        grad_gate_mix,
        jnp.concatenate([shares[0], shares[1]], axis=1)[None],
        shares[2][None],
    )


def solution(mesh):
    rows = P(("dp", "expert"), None)
    in_specs = (
        rows, rows, rows, rows,
        P("dp", None), P("dp", None), P("dp", None), P("dp", None), P("dp", None), P("dp"), P("dp"),
        P(), P("expert", None, None), P("expert", None, None), rows,
    )
    out_specs = (
        rows, rows, rows,
        P("dp", None), P("dp", None), P("dp", None), P("dp", None), P("dp", None), P("dp"), P("dp"),
        P(), P("expert", "dp", None), P("expert", "dp", None),
    )
    return jax.shard_map(
        per_device, mesh=mesh, in_specs=in_specs, out_specs=out_specs, check_vma=False
    )
```

profile of v0, /device:TPU:0, one launch (start us, length us, event | category | flops | bytes accessed | tf_op | source)
XLA Modules:
  0.0 368.3 jit_solution(3818222507864541473)
XLA Ops:
  0.7 0.8 fusion.16
  1.5 1.7 copy.58.routes_ref
  3.2 0.5 select_reduce_fusion.1
  4.0 0.5 multiply_sine_fusion
  4.8 1.0 copy.55.cos_ref
  5.8 1.0 copy.56.segc_ref
  6.9 0.6 pad_add_fusion.target_ref
  7.5 0.8 broadcast_multiply_fusion.sin_ref
  8.3 0.6 fusion.17
  8.9 0.8 pad.17.prev_ref
  9.8 0.9 fusion.2
  10.6 40.7 %gather_parts.1 = (bf16[8,2,48,3200]{3,2,1,0:T(8,128)(2,1)}, bf16[4,256,768]{2,1,0:T(8,128)(2,1)}) custom-call(bf16[2,48,3200]{2,1,0:T(8,128)(2,1)} %bitcast.74, bf16[1024,768]{1,0:T(8,128)(2,1)} %cot_ref.3, s32[2,1024]{1,0:T(2,128)} %pad_add_fusion.target_ref), custom_call_target="tpu_custom_call" | custom-call | flops 10000000000 | bytes 10000000 | tf_op jit(solution)/shard_map/gather_parts/pallas_call | solution.py:597
  51.4 26.9 %attend.1 = (bf16[3,1024,768]{2,1,0:T(8,128)(2,1)}, bf16[1024,768]{1,0:T(8,128)(2,1)}, bf16[1024,768]{1,0:T(8,128)(2,1)}, f32[16,1024]{1,0:T(8,128)}) custom-call(bf16[1024,768]{1,0:T(8,128)(2,1)} %tok_ref.5, bf16[768,3200]{1,0:T(8,128)(2,1)} %bitcast.53, bf16[768,3200]{1,0:T(8,128)(2,1)} %bitcast.54, bf16[768,3200]{1,0:T(8,128)(2,1)} %bitcast.55, ...), custom_call_target="tpu_custom_call" | custom-call | flops 12000000000 | bytes 16000000 | tf_op jit(solution)/shard_map/attend/pallas_call | solution.py:1263
  78.3 12.6 %middle.1 = (f32[1024,768]{1,0:T(8,128)}, f32[1024,128]{1,0:T(8,128)}, bf16[4,256,896]{2,1,0:T(8,128)(2,1)}) custom-call(bf16[1024,768]{1,0:T(8,128)(2,1)} %get-tuple-element.71.ao_ref, bf16[768,3200]{1,0:T(8,128)(2,1)} %bitcast.57, bf16[1024,768]{1,0:T(8,128)(2,1)} %tok_ref.5, bf16[768,3200]{1,0:T(8,128)(2,1)} %bitcast.58, f32[1024,128]{1,0:T(8,128)} %pad.17.prev_ref, ...), custom_call_target="tpu_custom_call" | custom-call | flops 3500000000 | bytes 10000000 | tf_op jit(solution)/shard_map/middle/pallas_call | solution.py:1285
  90.8 56.8 %exchange_experts.1 = (bf16[4,96,2048]{2,1,0:T(8,128)(2,1)}, bf16[4,96,2048]{2,1,0:T(8,128)(2,1)}, bf16[4,96,2048]{2,1,0:T(8,128)(2,1)}, bf16[4,96,2048]{2,1,0:T...) custom-call(bf16[4,256,896]{2,1,0:T(8,128)(2,1)} %get-tuple-element., ...), custom_call_target="tpu_custom_call" | custom-call | flops 28991029248 | bytes 40000000 | tf_op jit(solution)/shard_map/exchange_experts/pallas_call | solution.py:1092
  147.6 0.6 collective-permute-start
  148.2 1.5 collective-permute-start.1
  149.8 1.0 copy.60.target_ref
  150.9 0.6 pad.18.mix_ref
  151.5 0.6 fusion.3.ind_ref
  152.1 31.2 %combine.1 = (bf16[1024,768]{1,0:T(8,128)(2,1)}, f32[1024,8]{1,0:T(8,128)}, f32[1024,768]{1,0:T(8,128)}, bf16[1024,768]{1,0:T(8,128)(2,1)}, bf16[1024,768]{1,0:T...) custom-call(bf16[4,512,768]{2,1,0:T(8,128)(2,1)} %get-tuple-element., ...), custom_call_target="tpu_custom_call" | custom-call | flops 1000000 | bytes 100000 | tf_op jit(solution)/shard_map/combine/pallas_call | solution.py:1331
  183.3 1.9 collective-permute-done
  185.3 2.0 add_convert_fusion.1
  187.3 1.7 fusion.15
  189.2 3.1 collective-permute-start.5
  192.3 1.7 collective-permute-start.6
  193.9 0.7 collective-permute-start.4
  194.6 0.8 slice.56
  195.4 0.7 slice.57
  196.2 0.8 copy.65
  197.0 45.5 %attend_back.1 = (bf16[24,768,128]{2,1,0:T(8,128)(2,1)}, f32[1024,768]{1,0:T(8,128)}, f32[1,768]{1,0:T(1,128)}) custom-call(bf16[3,1024,768]{2,1,0:T(8,128)(2,1)} %get-tuple-element.87.qkv_ref, bf16[1024,768]{1,0:T(8,128)(2,1)} %get-tuple-element.91.grad_ref, f32[16,1024]{1,0:T(8,128)} %get-tuple-element.92.lse_ref, f32[16,1024]{1,0:T(8,128)} %get-tuple-element.93.delta_ref, ...), custom_call_target="tpu_custom_call" | custom-call | flops 1000000 | bytes 100000 | tf_op jit(solution)/shard_map/attend_back/pallas_call | solution.py:1374
  242.5 2.6 concatenate.14.minor_ref
  245.1 7.5 %collective-permute-done.4 = bf16[2,256,768]{2,1,0:T(8,128)(2,1)} collective-permute-done((bf16[2,256,768]{2,1,0:T(8,128)(2,1)}, bf16[2,256,768]{2,1,0:T(8,128)(2,1)}, u32[]{:S(2)}, u32[]{:S(2)}) %collective-permute-start.4) | collective-permute-done | bytes 786464 | tf_op jit(solution)/shard_map/ppermute | solution.py:464
  252.6 3.3 add_convert_fusion
  255.9 2.9 add_convert_fusion.2
  258.8 99.2 %reduce_parts.1 = (f32[3,32,2048]{2,1,0:T(8,128)}, f32[3,32,2048]{2,1,0:T(8,128)}, f32[8,32,768]{2,1,0:T(8,128)}, bf16[24,96,128]{2,1,0:T(8,128)(2,1)}, f32[24,768]{1,0:T(8,128)}) custom-call(bf16[4,3,32,2048]{3,2,1,0:T(8,128)(2,1)} %bitcast.65, bf16[4,3,32,2048]{3,2,1,0:T(8,128)(2,1)} %bitcast.66, bf16[3,3,32,2048]{3,2,1,0:T(8,128)(2,1)} %bitcast.23.risen_ref, ...), custom_call_target="tpu_custom_call" | custom-call | tf_op jit(solution)/shard_map/reduce_parts/pallas_call | solution.py:893
  358.0 1.2 convert_bitcast_fusion
  359.2 0.9 copy.64
  360.1 0.9 reshape.298
  361.1 1.0 slice.70
  362.1 0.7 slice.71
  362.9 0.6 slice.72
  363.5 0.6 slice.73
  364.1 0.5 slice_bitcast_fusion
  364.6 0.6 slice.74
  365.1 0.6 slice.67
  365.7 1.3 maximum_bitcast_fusion
  367.1 0.9 copy.69
  (69 shorter events, 1.1 us)
Async XLA Ops:
  0.6 3.1 copy-start.20
  0.7 3.1 copy-start.21
  0.7 3.1 copy-start.17
  0.7 3.1 copy-start.18
  0.7 3.1 copy-start.19
  4.5 1.3 copy-start.13
  4.6 2.3 copy-start.11
  4.8 3.6 copy-start.10
  4.8 3.6 copy-start.14
  5.8 3.9 %copy-start.8 = (bf16[96,2304]{1,0:T(8,128)(2,1)S(1)}, bf16[96,2304]{1,0:T(8,128)(2,1)}, u32[]{:S(2)}) copy-start(bf16[96,2304]{1,0:T(8,128)(2,1)} %param.19) | copy-start | bytes 1327108
  5.8 3.9 %copy-start.9 = (bf16[96,768]{1,0:T(8,128)(2,1)S(1)}, bf16[96,768]{1,0:T(8,128)(2,1)}, u32[]{:S(2)}) copy-start(bf16[96,768]{1,0:T(8,128)(2,1)} %param.20) | copy-start | bytes 442372
  147.6 37.6 %collective-permute-start = (bf16[4,96,2048]{2,1,0:T(8,128)(2,1)}, bf16[4,96,2048]{2,1,0:T(8,128)(2,1)}, u32[]{:S(2)}, u32[]{:S(2)}) collective-permute-start(bf16[4,96,2048]{2,1,0:T(8,128)(2,1)} %get-tuple-element.89), channel_id=1, source_target_pairs={{0,4},{4,0},{8,12},{12,8},{16,20},{20,16},{24,28},{28,24},{1,5},{5... | collective-permute-start | bytes 4718600 | tf_op jit(solution)/shard_map/ppermute | solution.py:464
  148.2 104.3 %collective-permute-start.1 = (bf16[4,96,2048]{2,1,0:T(8,128)(2,1)}, bf16[4,96,2048]{2,1,0:T(8,128)(2,1)}, u32[]{:S(2)}, u32[]{:S(2)}) collective-permute-start(bf16[4,96,2048]{2,1,0:T(8,128)(2,1)} %get-tuple-element.102), channel_id=1, source_target_pairs={{0,4},{4,0},{8,12},{12,8},{16,20},{20,16},{24,28},{28,24},{1,5},{5... | collective-permute-start | bytes 4718600 | tf_op jit(solution)/shard_map/ppermute | solution.py:464
  149.7 44.2 %collective-permute-start.2 = (bf16[2,256,768]{2,1,0:T(8,128)(2,1)}, bf16[2,256,768]{2,1,0:T(8,128)(2,1)}, u32[]{:S(2)}, u32[]{:S(2)}) collective-permute-start(bf16[2,256,768]{2,1,0:T(8,128)(2,1)} %get-tuple-element.104), channel_id=1, source_target_pairs={{0,8},{4,12},{8,0},{12,4},{16,24},{20,28},{24,16},{28,20},{1,9},{5... | collective-permute-start | bytes 2359304 | tf_op jit(solution)/shard_map/ppermute | solution.py:464
  152.1 33.2 %copy-start.2 = (bf16[4,96,2048]{2,1,0:T(8,128)(2,1)S(1)}, bf16[4,96,2048]{2,1,0:T(8,128)(2,1)}, u32[]{:S(2)}) copy-start(bf16[4,96,2048]{2,1,0:T(8,128)(2,1)} %get-tuple-element.99) | copy-start | bytes 4718596
  187.3 1.9 copy-start
  187.3 8.1 %copy-start.15 = (f32[8,128]{1,0:T(8,128)S(1)}, f32[8,128]{1,0:T(8,128)}, u32[]{:S(2)}) copy-start(f32[8,128]{1,0:T(8,128)} %get-tuple-element.121) | copy-start | bytes 12292
  187.3 8.9 %copy-start.7 = (f32[1024,8]{1,0:T(8,128)S(1)}, f32[1024,8]{1,0:T(8,128)}, u32[]{:S(2)}) copy-start(f32[1024,8]{1,0:T(8,128)} %get-tuple-element.155) | copy-start | bytes 98308
  189.2 63.3 %collective-permute-start.5 = (bf16[3,96,2048]{2,1,0:T(8,128)(2,1)}, bf16[3,96,2048]{2,1,0:T(8,128)(2,1)}, u32[]{:S(2)}, u32[]{:S(2)}) collective-permute-start(bf16[3,96,2048]{2,1,0:T(8,128)(2,1)} %get-tuple-element.169), channel_id=1, source_target_pairs={{0,8},{4,12},{1,9},{5,13},{2,10},{6,14},{3,11},{7,15}} | collective-permute-start | bytes 3538952 | tf_op jit(solution)/shard_map/ppermute | solution.py:1371
  192.3 60.3 %collective-permute-start.6 = (bf16[3,96,2048]{2,1,0:T(8,128)(2,1)}, bf16[3,96,2048]{2,1,0:T(8,128)(2,1)}, u32[]{:S(2)}, u32[]{:S(2)}) collective-permute-start(bf16[3,96,2048]{2,1,0:T(8,128)(2,1)} %get-tuple-element.168), channel_id=1, source_target_pairs={{24,16},{28,20},{25,17},{29,21},{26,18},{30,22},{27,19},{31,23}} | collective-permute-start | bytes 3538952 | tf_op jit(solution)/shard_map/ppermute | solution.py:1372
  193.9 51.1 %collective-permute-start.3 = (bf16[2,256,768]{2,1,0:T(8,128)(2,1)}, bf16[2,256,768]{2,1,0:T(8,128)(2,1)}, u32[]{:S(2)}, u32[]{:S(2)}) collective-permute-start(bf16[2,256,768]{2,1,0:T(8,128)(2,1)} %get-tuple-element.105), channel_id=1, source_target_pairs={{0,16},{4,20},{8,24},{12,28},{16,0},{20,4},{24,8},{28,12},{1,17},{... | collective-permute-start | bytes 2359304 | tf_op jit(solution)/shard_map/ppermute | solution.py:464
  193.9 58.6 %collective-permute-start.4 = (bf16[2,256,768]{2,1,0:T(8,128)(2,1)}, bf16[2,256,768]{2,1,0:T(8,128)(2,1)}, u32[]{:S(2)}, u32[]{:S(2)}) collective-permute-start(bf16[2,256,768]{2,1,0:T(8,128)(2,1)} %get-tuple-element.106), channel_id=1, source_target_pairs={{0,24},{4,28},{8,16},{12,20},{16,8},{20,12},{24,0},{28,4},{1,25},{... | collective-permute-start | bytes 2359304 | tf_op jit(solution)/shard_map/ppermute | solution.py:464
  197.0 45.5 %copy-start.16 = (f32[1,768]{1,0:T(1,128)S(1)}, f32[1,768]{1,0:T(1,128)}, u32[]{:S(2)}) copy-start(f32[1,768]{1,0:T(1,128)} %get-tuple-element.120) | copy-start | bytes 9220
  197.0 55.6 %copy-start.1 = (bf16[4,96,2048]{2,1,0:T(8,128)(2,1)S(1)}, bf16[4,96,2048]{2,1,0:T(8,128)(2,1)}, u32[]{:S(2)}) copy-start(bf16[4,96,2048]{2,1,0:T(8,128)(2,1)} %get-tuple-element.108) | copy-start | bytes 4718596
  252.6 3.3 copy-start.6
  361.1 1.7 copy-start.12
  361.1 4.7 %copy-start.4 = (f32[3,32,2048]{2,1,0:T(8,128)S(1)}, f32[3,32,2048]{2,1,0:T(8,128)}, u32[]{:S(2)}) copy-start(f32[3,32,2048]{2,1,0:T(8,128)} %get-tuple-element.124) | copy-start | bytes 2359300
  361.1 4.7 %copy-start.5 = (f32[3,32,2048]{2,1,0:T(8,128)S(1)}, f32[3,32,2048]{2,1,0:T(8,128)}, u32[]{:S(2)}) copy-start(f32[3,32,2048]{2,1,0:T(8,128)} %get-tuple-element.125) | copy-start | bytes 2359300
  365.7 1.4 copy-start.3
where the time goes:
time: 371 us; the launch traced here: 368 us
  Pallas kernels  313 us (84%)
  local copies, waits for them, and re-layouts  21.9 us (6%)
  other arithmetic  14.2 us (4%)
  waiting for transfers between devices  9.42 us (3%)
  starting transfers between devices  7.51 us (2%)
    pallas_call x1, Pallas kernels, reduce_parts(): pl.pallas_call(reduce_kernel, in_specs=[pl.BlockSpec(memory_space=pltpu.V...  99.2 us
    pallas_call x1, Pallas kernels, exchange_experts(): pl.pallas_call(exchange_kernel, in_specs=[anywhere] * 4, out_specs=[anywh...  56.8 us
    pallas_call x1, Pallas kernels, per_device(): pl.pallas_call(functools.partial(attend_back_kernel, kinds + 6), grid=(gr...  45.5 us
    pallas_call x1, Pallas kernels, gather_parts(): pl.pallas_call(gather_kernel, in_specs=[pl.BlockSpec(memory_space=pltpu.V...  40.7 us
    pallas_call x1, Pallas kernels, per_device(): pl.pallas_call(functools.partial(combine_kernel, kinds, experts), grid=(t...  31.2 us
    pallas_call x1, Pallas kernels, per_device(): pl.pallas_call(functools.partial(attend_kernel, kinds + 6), grid=(groups,...  26.9 us
    pallas_call x1, Pallas kernels, per_device(): pl.pallas_call(functools.partial(middle_kernel, kinds), grid=(1,), in_spe...  12.6 us
    ppermute x5, waiting for transfers between devices, over_parts(): return lax.ppermute(values, 'dp', [(d, d ^ bit) for d in range(8)])  9.42 us
  transfers between devices with their start and end apart: 7, of which 2 were waited for; matrix products, arithmetic and copies ran while one was open for 3% of the time, Pallas kernels for 21%

commit v1 on v0

--- a/solution.py
+++ b/solution.py
@@ -759,12 +759,35 @@
 
     half = core_in.shape[0]
     quarter = half // 2
-    core_weight = other_copy(0, weight_ref.at[pl.ds(half * (1 - core), half)], core_in, partner)
+    eighth = quarter // 2
+    core_weight = [
+        other_copy(
+            14 * order,
+            weight_ref.at[pl.ds(half * (1 - core) + quarter * which, quarter)],
+            core_in.at[pl.ds(quarter * which, quarter)],
+            partner,
+        )
+        for order, which in enumerate((1 - side, side))
+    ]
     core_small = other_copy(1, minor_ref, small_in.at[0], partner)
-    side_weight = other_copy(2, core_sum.at[pl.ds(quarter * (1 - side), quarter)], side_in, beside)
+    side_weight = [
+        other_copy(
+            2 + 13 * order,
+            core_sum.at[pl.ds(quarter * (1 - side) + eighth * order, eighth)],
+            side_in.at[pl.ds(eighth * order, eighth)],
+            beside,
+        )
+        for order in range(2)
+    ]
     side_small = other_copy(3, small_sum.at[0], small_in.at[1], beside)
     cross_weight = [
-        other_copy(4 + z, side_sum.at[:, 2 * z + 1 - flank], cross_in.at[z], across)
+        other_copy(
+            4 + 12 * order + z,
+            side_sum.at[pl.ds(eighth * order, eighth), 2 * z + 1 - flank],
+            cross_in.at[z, pl.ds(eighth * order, eighth)],
+            across,
+        )
+        for order in range(2)
         for z in range(4)
     ]
     cross_small = other_copy(8, small_sum.at[1], small_in.at[2], across)
@@ -777,7 +800,8 @@
     core_back = other_copy(12, own_half, own_half, partner)
 
     pair_copy = other_copy(13, pair_ref.at[1 - flank], pair_in, across)
-    core_weight.start()
+    for copy in core_weight:
+        copy.start()
     core_small.start()
     pair_copy.start()
     for turn_index in range(3):
@@ -795,22 +819,35 @@
 
     for turn_index in range(2):
         early(turn_index)
-    core_weight.wait_recv()
+    for order, which in enumerate((1 - side, side)):
+        core_weight[order].wait_recv()
+        add_planes(
+            core_sum.at[pl.ds(quarter * which, quarter)],
+            weight_ref.at[pl.ds(half * core + quarter * which, quarter)],
+            core_in.at[pl.ds(quarter * which, quarter)],
+        )
+        if order == 0:
+            for copy in side_weight:
+                copy.start()
     core_small.wait_recv()
-    add_planes(core_sum, weight_ref.at[pl.ds(half * core, half)], core_in)
     small_sum[0] = minor_ref[...] + small_in[0]
-    side_weight.start()
     side_small.start()
     for piece in (0, 1):
         relay(piece, 0)
     pair_copy.wait_recv()
     add_planes(down_out, pair_ref.at[flank], pair_in)
-    side_weight.wait_recv()
+    for order in range(2):
+        span = pl.ds(eighth * order, eighth)
+        side_weight[order].wait_recv()
+        add_planes(
+            side_sum.at[span],
+            core_sum.at[pl.ds(quarter * side + eighth * order, eighth)],
+            side_in.at[span],
+        )
+        for copy in cross_weight[4 * order : 4 * order + 4]:
+            copy.start()
     side_small.wait_recv()
-    add_planes(side_sum, core_sum.at[pl.ds(quarter * side, quarter)], side_in)
     small_sum[1] = small_sum[0] + small_in[1]
-    for copy in cross_weight:
-        copy.start()
     cross_small.start()
     for piece in (0, 1):
         relay(piece, 1)
@@ -836,29 +873,30 @@
     for turn_index in range(2):
         relay(2, turn_index)
 
-    @pl.when(here > 0)
-    def _():
-        rise_small.wait_recv()
-        small_sum[3] = small_sum[2] + small_in[3]
-
-    @pl.when((here > 0) & (here < 3))
-    def _():
-        rise_small.start()
-
-    @pl.when(here < 3)
-    def _():
-        fall_small.wait_recv()
-        small_sum[4] = small_sum[2] + small_in[4]
-
-    @pl.when((here > 0) & (here < 3))
-    def _():
-        fall_small.start()
-
-    minor_out[...] = small_sum[3] + small_sum[4] - small_sum[2]
     finish(2, line_sum_ref)
     for index in range(quarter):
         weight_out[mine + index] = line_sum_ref[index]
     side_back.start()
+
+    @pl.when(here > 0)
+    def _():
+        rise_small.wait_recv()
+        small_sum[3] = small_sum[2] + small_in[3]
+
+    @pl.when((here > 0) & (here < 3))
+    def _():
+        rise_small.start()
+
+    @pl.when(here < 3)
+    def _():
+        fall_small.wait_recv()
+        small_sum[4] = small_sum[2] + small_in[4]
+
+    @pl.when((here > 0) & (here < 3))
+    def _():
+        fall_small.start()
+
+    minor_out[...] = small_sum[3] + small_sum[4] - small_sum[2]
     finish(0, gate_out)
     side_back.wait_recv()
     core_back.start()
@@ -866,7 +904,7 @@
     core_back.wait_recv()
     for piece in range(3):
         drain(piece)
-    for copy in (core_weight, core_small, side_weight, side_small, *cross_weight, cross_small,
+    for copy in (*core_weight, core_small, *side_weight, side_small, *cross_weight, cross_small,
                  side_back, core_back, pair_copy):
         copy.wait_send()
 
@@ -914,8 +952,8 @@
             pltpu.VMEM((5,) + minor.shape, F32),
             pltpu.SemaphoreType.DMA((3, 3, 2)),
             pltpu.SemaphoreType.DMA((3, 3, 2)),
-            pltpu.SemaphoreType.DMA((14,)),
-            pltpu.SemaphoreType.DMA((14,)),
+            pltpu.SemaphoreType.DMA((20,)),
+            pltpu.SemaphoreType.DMA((20,)),
         ],
         compiler_params=params(collective_id=1, has_side_effects=True),
         name="reduce_parts",

time: 371 us -> 364 us (0.981)
  Pallas kernels: 313 us -> 305 us
    pallas_call x1, Pallas kernels: 99.2 us -> 91.6 us  [reduce_parts(): pl.pallas_call(reduce_kernel, in_specs=[pl.BlockSpec(memory_space=pltpu.V...]
where the time goes in v1:
time: 364 us; the launch traced here: 361 us
  Pallas kernels  305 us (84%)
  local copies, waits for them, and re-layouts  21.9 us (6%)
  other arithmetic  14.2 us (4%)
  waiting for transfers between devices  9.42 us (3%)
  starting transfers between devices  7.51 us (2%)
    pallas_call x1, Pallas kernels, reduce_parts(): pl.pallas_call(reduce_kernel, in_specs=[pl.BlockSpec(memory_space=pltpu.V...  91.6 us
    pallas_call x1, Pallas kernels, exchange_experts(): pl.pallas_call(exchange_kernel, in_specs=[anywhere] * 4, out_specs=[anywh...  56.8 us
    pallas_call x1, Pallas kernels, per_device(): pl.pallas_call(functools.partial(attend_back_kernel, kinds + 6), grid=(gr...  45.5 us
    pallas_call x1, Pallas kernels, gather_parts(): pl.pallas_call(gather_kernel, in_specs=[pl.BlockSpec(memory_space=pltpu.V...  40.7 us
    pallas_call x1, Pallas kernels, per_device(): pl.pallas_call(functools.partial(combine_kernel, kinds, experts), grid=(t...  31.2 us
    pallas_call x1, Pallas kernels, per_device(): pl.pallas_call(functools.partial(attend_kernel, kinds + 6), grid=(groups,...  26.9 us
    pallas_call x1, Pallas kernels, per_device(): pl.pallas_call(functools.partial(middle_kernel, kinds), grid=(1,), in_spe...  12.6 us
    ppermute x5, waiting for transfers between devices, over_parts(): return lax.ppermute(values, 'dp', [(d, d ^ bit) for d in range(8)])  9.42 us
  transfers between devices with their start and end apart: 7, of which 2 were waited for; matrix products, arithmetic and copies ran while one was open for 3% of the time, Pallas kernels for 21%

profile of v1, /device:TPU:0, one launch (start us, length us, event | category | flops | bytes accessed | tf_op | source)
XLA Modules:
  0.0 360.7 jit_solution(12090758995318062062)
XLA Ops:
  0.7 0.8 fusion.16
  1.5 1.7 copy.58.routes_ref
  3.2 0.5 select_reduce_fusion.1
  4.0 0.5 multiply_sine_fusion
  4.8 1.0 copy.55.cos_ref
  5.8 1.0 copy.56.segc_ref
  6.9 0.6 pad_add_fusion.target_ref
  7.5 0.8 broadcast_multiply_fusion.sin_ref
  8.3 0.6 fusion.17
  8.9 0.8 pad.17.prev_ref
  9.8 0.9 fusion.2
  10.6 40.7 %gather_parts.1 = (bf16[8,2,48,3200]{3,2,1,0:T(8,128)(2,1)}, bf16[4,256,768]{2,1,0:T(8,128)(2,1)}) custom-call(bf16[2,48,3200]{2,1,0:T(8,128)(2,1)} %bitcast.74, bf16[1024,768]{1,0:T(8,128)(2,1)} %cot_ref.3, s32[2,1024]{1,0:T(2,128)} %pad_add_fusion.target_ref), custom_call_target="tpu_custom_call" | custom-call | flops 10000000000 | bytes 10000000 | tf_op jit(solution)/shard_map/gather_parts/pallas_call | solution.py:597
  51.4 26.9 %attend.1 = (bf16[3,1024,768]{2,1,0:T(8,128)(2,1)}, bf16[1024,768]{1,0:T(8,128)(2,1)}, bf16[1024,768]{1,0:T(8,128)(2,1)}, f32[16,1024]{1,0:T(8,128)}) custom-call(bf16[1024,768]{1,0:T(8,128)(2,1)} %tok_ref.5, bf16[768,3200]{1,0:T(8,128)(2,1)} %bitcast.53, bf16[768,3200]{1,0:T(8,128)(2,1)} %bitcast.54, bf16[768,3200]{1,0:T(8,128)(2,1)} %bitcast.55, ...), custom_call_target="tpu_custom_call" | custom-call | flops 12000000000 | bytes 16000000 | tf_op jit(solution)/shard_map/attend/pallas_call | solution.py:1301
  78.3 12.6 %middle.1 = (f32[1024,768]{1,0:T(8,128)}, f32[1024,128]{1,0:T(8,128)}, bf16[4,256,896]{2,1,0:T(8,128)(2,1)}) custom-call(bf16[1024,768]{1,0:T(8,128)(2,1)} %get-tuple-element.71.ao_ref, bf16[768,3200]{1,0:T(8,128)(2,1)} %bitcast.57, bf16[1024,768]{1,0:T(8,128)(2,1)} %tok_ref.5, bf16[768,3200]{1,0:T(8,128)(2,1)} %bitcast.58, f32[1024,128]{1,0:T(8,128)} %pad.17.prev_ref, ...), custom_call_target="tpu_custom_call" | custom-call | flops 3500000000 | bytes 10000000 | tf_op jit(solution)/shard_map/middle/pallas_call | solution.py:1323
  90.8 56.8 %exchange_experts.1 = (bf16[4,96,2048]{2,1,0:T(8,128)(2,1)}, bf16[4,96,2048]{2,1,0:T(8,128)(2,1)}, bf16[4,96,2048]{2,1,0:T(8,128)(2,1)}, bf16[4,96,2048]{2,1,0:T...) custom-call(bf16[4,256,896]{2,1,0:T(8,128)(2,1)} %get-tuple-element., ...), custom_call_target="tpu_custom_call" | custom-call | flops 28991029248 | bytes 40000000 | tf_op jit(solution)/shard_map/exchange_experts/pallas_call | solution.py:1130
  147.6 0.6 collective-permute-start
  148.2 1.5 collective-permute-start.1
  149.8 1.0 copy.60.target_ref
  150.9 0.6 pad.18.mix_ref
  151.5 0.6 fusion.3.ind_ref
  152.1 31.2 %combine.1 = (bf16[1024,768]{1,0:T(8,128)(2,1)}, f32[1024,8]{1,0:T(8,128)}, f32[1024,768]{1,0:T(8,128)}, bf16[1024,768]{1,0:T(8,128)(2,1)}, bf16[1024,768]{1,0:T...) custom-call(bf16[4,512,768]{2,1,0:T(8,128)(2,1)} %get-tuple-element., ...), custom_call_target="tpu_custom_call" | custom-call | flops 1000000 | bytes 100000 | tf_op jit(solution)/shard_map/combine/pallas_call | solution.py:1369
  183.3 1.9 collective-permute-done
  185.3 2.0 add_convert_fusion.1
  187.3 1.7 fusion.15
  189.2 3.1 collective-permute-start.5
  192.3 1.7 collective-permute-start.6
  193.9 0.7 collective-permute-start.4
  194.6 0.8 slice.56
  195.4 0.7 slice.57
  196.2 0.8 copy.65
  197.0 45.5 %attend_back.1 = (bf16[24,768,128]{2,1,0:T(8,128)(2,1)}, f32[1024,768]{1,0:T(8,128)}, f32[1,768]{1,0:T(1,128)}) custom-call(bf16[3,1024,768]{2,1,0:T(8,128)(2,1)} %get-tuple-element.87.qkv_ref, bf16[1024,768]{1,0:T(8,128)(2,1)} %get-tuple-element.91.grad_ref, f32[16,1024]{1,0:T(8,128)} %get-tuple-element.92.lse_ref, f32[16,1024]{1,0:T(8,128)} %get-tuple-element.93.delta_ref, ...), custom_call_target="tpu_custom_call" | custom-call | flops 1000000 | bytes 100000 | tf_op jit(solution)/shard_map/attend_back/pallas_call | solution.py:1412
  242.5 2.6 concatenate.14.minor_ref
  245.1 7.5 %collective-permute-done.4 = bf16[2,256,768]{2,1,0:T(8,128)(2,1)} collective-permute-done((bf16[2,256,768]{2,1,0:T(8,128)(2,1)}, bf16[2,256,768]{2,1,0:T(8,128)(2,1)}, u32[]{:S(2)}, u32[]{:S(2)}) %collective-permute-start.4) | collective-permute-done | bytes 786464 | tf_op jit(solution)/shard_map/ppermute | solution.py:464
  252.6 3.3 add_convert_fusion
  255.9 2.9 add_convert_fusion.2
  258.8 91.6 %reduce_parts.1 = (f32[3,32,2048]{2,1,0:T(8,128)}, f32[3,32,2048]{2,1,0:T(8,128)}, f32[8,32,768]{2,1,0:T(8,128)}, bf16[24,96,128]{2,1,0:T(8,128)(2,1)}, f32[24,768]{1,0:T(8,128)}) custom-call(bf16[4,3,32,2048]{3,2,1,0:T(8,128)(2,1)} %bitcast.65, bf16[4,3,32,2048]{3,2,1,0:T(8,128)(2,1)} %bitcast.66, bf16[3,3,32,2048]{3,2,1,0:T(8,128)(2,1)} %bitcast.23.risen_ref, ...), custom_call_target="tpu_custom_call" | custom-call | tf_op jit(solution)/shard_map/reduce_parts/pallas_call | solution.py:931
  350.4 1.2 convert_bitcast_fusion
  351.6 0.9 copy.64
  352.5 0.9 reshape.298
  353.5 1.0 slice.70
  354.4 0.7 slice.71
  355.3 0.6 slice.72
  355.9 0.6 slice.73
  356.4 0.5 slice_bitcast_fusion
  357.0 0.6 slice.74
  357.5 0.6 slice.67
  358.1 1.3 maximum_bitcast_fusion
  359.5 0.9 copy.69
  (69 shorter events, 1.1 us)
Async XLA Ops:
  0.6 3.1 copy-start.20
  0.7 3.1 copy-start.21
  0.7 3.1 copy-start.17
  0.7 3.1 copy-start.18
  0.7 3.1 copy-start.19
  4.5 1.3 copy-start.13
  4.6 2.3 copy-start.11
  4.8 3.6 copy-start.10
  4.8 3.6 copy-start.14
  5.8 3.9 %copy-start.8 = (bf16[96,2304]{1,0:T(8,128)(2,1)S(1)}, bf16[96,2304]{1,0:T(8,128)(2,1)}, u32[]{:S(2)}) copy-start(bf16[96,2304]{1,0:T(8,128)(2,1)} %param.19) | copy-start | bytes 1327108
  5.8 3.9 %copy-start.9 = (bf16[96,768]{1,0:T(8,128)(2,1)S(1)}, bf16[96,768]{1,0:T(8,128)(2,1)}, u32[]{:S(2)}) copy-start(bf16[96,768]{1,0:T(8,128)(2,1)} %param.20) | copy-start | bytes 442372
  147.6 37.6 %collective-permute-start = (bf16[4,96,2048]{2,1,0:T(8,128)(2,1)}, bf16[4,96,2048]{2,1,0:T(8,128)(2,1)}, u32[]{:S(2)}, u32[]{:S(2)}) collective-permute-start(bf16[4,96,2048]{2,1,0:T(8,128)(2,1)} %get-tuple-element.89), channel_id=1, source_target_pairs={{0,4},{4,0},{8,12},{12,8},{16,20},{20,16},{24,28},{28,24},{1,5},{5... | collective-permute-start | bytes 4718600 | tf_op jit(solution)/shard_map/ppermute | solution.py:464
  148.2 104.3 %collective-permute-start.1 = (bf16[4,96,2048]{2,1,0:T(8,128)(2,1)}, bf16[4,96,2048]{2,1,0:T(8,128)(2,1)}, u32[]{:S(2)}, u32[]{:S(2)}) collective-permute-start(bf16[4,96,2048]{2,1,0:T(8,128)(2,1)} %get-tuple-element.102), channel_id=1, source_target_pairs={{0,4},{4,0},{8,12},{12,8},{16,20},{20,16},{24,28},{28,24},{1,5},{5... | collective-permute-start | bytes 4718600 | tf_op jit(solution)/shard_map/ppermute | solution.py:464
  149.7 44.2 %collective-permute-start.2 = (bf16[2,256,768]{2,1,0:T(8,128)(2,1)}, bf16[2,256,768]{2,1,0:T(8,128)(2,1)}, u32[]{:S(2)}, u32[]{:S(2)}) collective-permute-start(bf16[2,256,768]{2,1,0:T(8,128)(2,1)} %get-tuple-element.104), channel_id=1, source_target_pairs={{0,8},{4,12},{8,0},{12,4},{16,24},{20,28},{24,16},{28,20},{1,9},{5... | collective-permute-start | bytes 2359304 | tf_op jit(solution)/shard_map/ppermute | solution.py:464
  152.1 33.2 %copy-start.2 = (bf16[4,96,2048]{2,1,0:T(8,128)(2,1)S(1)}, bf16[4,96,2048]{2,1,0:T(8,128)(2,1)}, u32[]{:S(2)}) copy-start(bf16[4,96,2048]{2,1,0:T(8,128)(2,1)} %get-tuple-element.99) | copy-start | bytes 4718596
  187.3 1.9 copy-start
  187.3 8.1 %copy-start.15 = (f32[8,128]{1,0:T(8,128)S(1)}, f32[8,128]{1,0:T(8,128)}, u32[]{:S(2)}) copy-start(f32[8,128]{1,0:T(8,128)} %get-tuple-element.121) | copy-start | bytes 12292
  187.3 8.9 %copy-start.7 = (f32[1024,8]{1,0:T(8,128)S(1)}, f32[1024,8]{1,0:T(8,128)}, u32[]{:S(2)}) copy-start(f32[1024,8]{1,0:T(8,128)} %get-tuple-element.155) | copy-start | bytes 98308
  189.2 63.3 %collective-permute-start.5 = (bf16[3,96,2048]{2,1,0:T(8,128)(2,1)}, bf16[3,96,2048]{2,1,0:T(8,128)(2,1)}, u32[]{:S(2)}, u32[]{:S(2)}) collective-permute-start(bf16[3,96,2048]{2,1,0:T(8,128)(2,1)} %get-tuple-element.169), channel_id=1, source_target_pairs={{0,8},{4,12},{1,9},{5,13},{2,10},{6,14},{3,11},{7,15}} | collective-permute-start | bytes 3538952 | tf_op jit(solution)/shard_map/ppermute | solution.py:1409
  192.3 60.3 %collective-permute-start.6 = (bf16[3,96,2048]{2,1,0:T(8,128)(2,1)}, bf16[3,96,2048]{2,1,0:T(8,128)(2,1)}, u32[]{:S(2)}, u32[]{:S(2)}) collective-permute-start(bf16[3,96,2048]{2,1,0:T(8,128)(2,1)} %get-tuple-element.168), channel_id=1, source_target_pairs={{24,16},{28,20},{25,17},{29,21},{26,18},{30,22},{27,19},{31,23}} | collective-permute-start | bytes 3538952 | tf_op jit(solution)/shard_map/ppermute | solution.py:1410
  193.9 51.1 %collective-permute-start.3 = (bf16[2,256,768]{2,1,0:T(8,128)(2,1)}, bf16[2,256,768]{2,1,0:T(8,128)(2,1)}, u32[]{:S(2)}, u32[]{:S(2)}) collective-permute-start(bf16[2,256,768]{2,1,0:T(8,128)(2,1)} %get-tuple-element.105), channel_id=1, source_target_pairs={{0,16},{4,20},{8,24},{12,28},{16,0},{20,4},{24,8},{28,12},{1,17},{... | collective-permute-start | bytes 2359304 | tf_op jit(solution)/shard_map/ppermute | solution.py:464
  193.9 58.6 %collective-permute-start.4 = (bf16[2,256,768]{2,1,0:T(8,128)(2,1)}, bf16[2,256,768]{2,1,0:T(8,128)(2,1)}, u32[]{:S(2)}, u32[]{:S(2)}) collective-permute-start(bf16[2,256,768]{2,1,0:T(8,128)(2,1)} %get-tuple-element.106), channel_id=1, source_target_pairs={{0,24},{4,28},{8,16},{12,20},{16,8},{20,12},{24,0},{28,4},{1,25},{... | collective-permute-start | bytes 2359304 | tf_op jit(solution)/shard_map/ppermute | solution.py:464
  197.0 45.5 %copy-start.16 = (f32[1,768]{1,0:T(1,128)S(1)}, f32[1,768]{1,0:T(1,128)}, u32[]{:S(2)}) copy-start(f32[1,768]{1,0:T(1,128)} %get-tuple-element.120) | copy-start | bytes 9220
  197.0 55.6 %copy-start.1 = (bf16[4,96,2048]{2,1,0:T(8,128)(2,1)S(1)}, bf16[4,96,2048]{2,1,0:T(8,128)(2,1)}, u32[]{:S(2)}) copy-start(bf16[4,96,2048]{2,1,0:T(8,128)(2,1)} %get-tuple-element.108) | copy-start | bytes 4718596
  252.6 3.3 copy-start.6
  353.4 1.7 copy-start.12
  353.5 4.7 %copy-start.4 = (f32[3,32,2048]{2,1,0:T(8,128)S(1)}, f32[3,32,2048]{2,1,0:T(8,128)}, u32[]{:S(2)}) copy-start(f32[3,32,2048]{2,1,0:T(8,128)} %get-tuple-element.124) | copy-start | bytes 2359300
  353.5 4.7 %copy-start.5 = (f32[3,32,2048]{2,1,0:T(8,128)S(1)}, f32[3,32,2048]{2,1,0:T(8,128)}, u32[]{:S(2)}) copy-start(f32[3,32,2048]{2,1,0:T(8,128)} %get-tuple-element.125) | copy-start | bytes 2359300
  358.1 1.4 copy-start.3

commit v2 on v1

--- a/solution.py
+++ b/solution.py
@@ -528,12 +528,20 @@
         def _():
             copy(me, core, route, part_ref.at[core]).start()
     tokens = cot_ref.shape[0]
-    for slot, peer in enumerate(peers):
+
+    @pl.loop(0, 4)
+    def _(slot):
+        turn_core, turn_side = (slot + 1) // 2 % 2, 1 - slot // 2
+        peer = (
+            core + turn_core - 2 * core * turn_core
+            + 2 * (side + turn_side - 2 * side * turn_side)
+        )
         slots = iota((CAP, tokens), 0) + peer * CAP
         hot = (target_ref[0:1, :] == slots) | (target_ref[1:2, :] == slots)
         outgoing[slot] = nn(hot.astype(F32).astype(BF16), cot_ref[...]).astype(BF16)
-        if slot > 0:
-            row_copy(slot - 1).start()
+
+    for slot in range(3):
+        row_copy(slot).start()
     own_rows = pltpu.make_async_copy(outgoing.at[3], rows_ref.at[owner], own_sem)
     own_rows.start()
     for distance in range(1, 5):
@@ -919,8 +927,8 @@
 
 def reduce_parts(kept, down, weights, minor):
     gate, up = kept[:2]
-    kept = [piece.reshape(-1, piece.shape[1] // 32, 32, piece.shape[2]) for piece in kept]
-    pair = down.reshape(2, down.shape[1] // 32, 32, down.shape[2])
+    kept = [piece.reshape(-1, piece.shape[1] // 8, 8, piece.shape[2]) for piece in kept]
+    pair = down.reshape(2, down.shape[1] // 8, 8, down.shape[2])
     blocks, width, lanes = weights.shape
     rows = width // 8
     plane = (rows, lanes)
@@ -989,18 +997,25 @@
     tiles = ff // FF_TILE
     greet([(always, {"expert": peer}) for peer in peers[1:]])
 
+    def peer_of(slot):
+        turn_core, turn_side = slot // 2, 1 - slot // 3
+        return (
+            core + turn_core - 2 * core * turn_core
+            + 2 * (side + turn_side - 2 * side * turn_side)
+        )
+
     def token_copy(slot):
         return pltpu.make_async_remote_copy(
-            src_ref=send_ref.at[peers[slot]], dst_ref=recv.at[slot],
+            src_ref=send_ref.at[peer_of(slot)], dst_ref=recv.at[slot],
             send_sem=token_send.at[slot], recv_sem=token_recv.at[slot],
-            device_id={"expert": peers[slot]}, device_id_type=MESH,
+            device_id={"expert": peer_of(slot)}, device_id_type=MESH,
         )
 
     def back_copy(slot):
         return pltpu.make_async_remote_copy(
             src_ref=ret.at[slot], dst_ref=return_out.at[me],
             send_sem=back_send.at[slot], recv_sem=back_recv.at[slot],
-            device_id={"expert": peers[slot]}, device_id_type=MESH,
+            device_id={"expert": peer_of(slot)}, device_id_type=MESH,
         )
 
     def tile_slice(tile):
@@ -1057,9 +1072,12 @@
         @pl.loop(0, tiles)
         def _(tile):
             cols = tile_slice(tile)
-            if slot == 0:
+
+            @pl.when(slot == 0)
+            def _():
                 for copy in weight_copies(tile):
                     copy.wait()
+
             token = recv[slot, :, 0:width]
             gate = nn(token, gate_w[:, cols])
             up = nn(token, up_w[:, cols])
@@ -1077,15 +1095,27 @@
 
         ret[slot, 0:CAP, :] = out_acc[...].astype(BF16)
         ret[slot, CAP:, :] = row_acc[...].astype(BF16)
-        turned[:, slot * CAP : (slot + 1) * CAP] = recv[slot, :, 0:width].T
+        turned[:, pl.ds(pl.multiple_of(slot * CAP, CAP), CAP)] = recv[slot, :, 0:width].T
 
     own_back = pltpu.make_async_copy(ret.at[0], return_out.at[me], own_sem)
-    work(0)
-    own_back.start()
-    for slot in (1, 2, 3):
-        token_copy(slot).wait_recv()
+
+
+    @pl.loop(0, 4)
+    def _(slot):
+        @pl.when(slot > 0)
+        def _():
+            token_copy(slot).wait_recv()
+
         work(slot)
-        back_copy(slot).start()
+
+        @pl.when(slot > 0)
+        def _():
+            back_copy(slot).start()
+
+        @pl.when(slot == 0)
+        def _():
+            own_back.start()
+
     total = 4 * CAP
 
     @pl.loop(0, tiles)

time: 364 us -> 361 us (level)
    reshape x0 -> x2, other arithmetic: none -> 6.19 us  [the longest x1 3.29 us: reduce_parts(): piece.reshape(-1, piece.shape[1] // 8, 8, piece.shape[2])]
where the time goes in v2:
time: 361 us
  Pallas kernels  305 us (84%)
  local copies, waits for them, and re-layouts  21.9 us (6%)
  other arithmetic  14.2 us (4%)
  waiting for transfers between devices  9.67 us (3%)
  starting transfers between devices  7.51 us (2%)
    pallas_call x1, Pallas kernels, reduce_parts(): pl.pallas_call(reduce_kernel, in_specs=[pl.BlockSpec(memory_space=pltpu.V...  92 us
    pallas_call x1, Pallas kernels, exchange_experts(): pl.pallas_call(exchange_kernel, in_specs=[anywhere] * 4, out_specs=[anywh...  56.8 us
    pallas_call x1, Pallas kernels, per_device(): pl.pallas_call(functools.partial(attend_back_kernel, kinds + 6), grid=(gr...  45.2 us
    pallas_call x1, Pallas kernels, gather_parts(): pl.pallas_call(gather_kernel, in_specs=[pl.BlockSpec(memory_space=pltpu.V...  40.7 us
    pallas_call x1, Pallas kernels, per_device(): pl.pallas_call(functools.partial(combine_kernel, kinds, experts), grid=(t...  31.2 us
    pallas_call x1, Pallas kernels, per_device(): pl.pallas_call(functools.partial(attend_kernel, kinds + 6), grid=(groups,...  26.9 us
    pallas_call x1, Pallas kernels, per_device(): pl.pallas_call(functools.partial(middle_kernel, kinds), grid=(1,), in_spe...  12.6 us
    ppermute x5, waiting for transfers between devices, over_parts(): return lax.ppermute(values, 'dp', [(d, d ^ bit) for d in range(8)])  9.66 us
  transfers between devices with their start and end apart: 7, of which 2 were waited for; matrix products, arithmetic and copies ran while one was open for 3% of the time, Pallas kernels for 21%

profile of v2, /device:TPU:0, one launch (start us, length us, event | category | flops | bytes accessed | tf_op | source)
XLA Modules:
  0.0 360.8 jit_solution(16019218301992148108)
XLA Ops:
  0.7 0.8 fusion.18
  1.5 1.7 copy.58.routes_ref
  3.2 0.5 select_reduce_fusion.1
  4.0 0.5 multiply_sine_fusion
  4.8 1.0 copy.55.cos_ref
  5.8 1.0 copy.56.segc_ref
  6.9 0.6 pad_add_fusion.target_ref
  7.5 0.8 broadcast_multiply_fusion.sin_ref
  8.3 0.6 fusion.19
  8.9 0.8 pad.17.prev_ref
  9.8 0.9 fusion.4
  10.6 40.7 %gather_parts.1 = (bf16[8,2,48,3200]{3,2,1,0:T(8,128)(2,1)}, bf16[4,256,768]{2,1,0:T(8,128)(2,1)}) custom-call(bf16[2,48,3200]{2,1,0:T(8,128)(2,1)} %bitcast.74, bf16[1024,768]{1,0:T(8,128)(2,1)} %cot_ref.3, s32[2,1024]{1,0:T(2,128)} %pad_add_fusion.target_ref), custom_call_target="tpu_custom_call" | custom-call | flops 10000000000 | bytes 10000000 | tf_op jit(solution)/shard_map/gather_parts/pallas_call | solution.py:605
  51.4 26.9 %attend.1 = (bf16[3,1024,768]{2,1,0:T(8,128)(2,1)}, bf16[1024,768]{1,0:T(8,128)(2,1)}, bf16[1024,768]{1,0:T(8,128)(2,1)}, f32[16,1024]{1,0:T(8,128)}) custom-call(bf16[1024,768]{1,0:T(8,128)(2,1)} %tok_ref.5, bf16[768,3200]{1,0:T(8,128)(2,1)} %bitcast.55, bf16[768,3200]{1,0:T(8,128)(2,1)} %bitcast.56, bf16[768,3200]{1,0:T(8,128)(2,1)} %bitcast.57, ...), custom_call_target="tpu_custom_call" | custom-call | flops 12000000000 | bytes 16000000 | tf_op jit(solution)/shard_map/attend/pallas_call | solution.py:1331
  78.3 12.6 %middle.1 = (f32[1024,768]{1,0:T(8,128)}, f32[1024,128]{1,0:T(8,128)}, bf16[4,256,896]{2,1,0:T(8,128)(2,1)}) custom-call(bf16[1024,768]{1,0:T(8,128)(2,1)} %get-tuple-element.71.ao_ref, bf16[768,3200]{1,0:T(8,128)(2,1)} %bitcast.59, bf16[1024,768]{1,0:T(8,128)(2,1)} %tok_ref.5, bf16[768,3200]{1,0:T(8,128)(2,1)} %bitcast.60, f32[1024,128]{1,0:T(8,128)} %pad.17.prev_ref, ...), custom_call_target="tpu_custom_call" | custom-call | flops 3500000000 | bytes 10000000 | tf_op jit(solution)/shard_map/middle/pallas_call | solution.py:1353
  90.8 56.8 %exchange_experts.1 = (bf16[4,96,2048]{2,1,0:T(8,128)(2,1)}, bf16[4,96,2048]{2,1,0:T(8,128)(2,1)}, bf16[4,96,2048]{2,1,0:T(8,128)(2,1)}, bf16[4,96,2048]{2,1,0:T...) custom-call(bf16[4,256,896]{2,1,0:T(8,128)(2,1)} %get-tuple-element., ...), custom_call_target="tpu_custom_call" | custom-call | flops 28991029248 | bytes 40000000 | tf_op jit(solution)/shard_map/exchange_experts/pallas_call | solution.py:1160
  147.6 0.6 collective-permute-start
  148.2 1.5 collective-permute-start.1
  149.8 1.0 copy.60.target_ref
  150.9 0.6 pad.18.mix_ref
  151.5 0.6 fusion.5.ind_ref
  152.1 31.2 %combine.1 = (bf16[1024,768]{1,0:T(8,128)(2,1)}, f32[1024,8]{1,0:T(8,128)}, f32[1024,768]{1,0:T(8,128)}, bf16[1024,768]{1,0:T(8,128)(2,1)}, bf16[1024,768]{1,0:T...) custom-call(bf16[4,512,768]{2,1,0:T(8,128)(2,1)} %get-tuple-element., ...), custom_call_target="tpu_custom_call" | custom-call | flops 1000000 | bytes 100000 | tf_op jit(solution)/shard_map/combine/pallas_call | solution.py:1399
  183.3 1.9 collective-permute-done
  185.3 2.0 add_convert_fusion.1
  187.3 1.7 fusion.17
  189.2 3.1 collective-permute-start.5
  192.3 1.7 collective-permute-start.6
  193.9 0.7 collective-permute-start.4
  194.6 0.8 slice.56
  195.4 0.7 slice.57
  196.2 0.8 copy.65
  197.0 45.2 %attend_back.1 = (bf16[24,768,128]{2,1,0:T(8,128)(2,1)}, f32[1024,768]{1,0:T(8,128)}, f32[1,768]{1,0:T(1,128)}) custom-call(bf16[3,1024,768]{2,1,0:T(8,128)(2,1)} %get-tuple-element.87.qkv_ref, bf16[1024,768]{1,0:T(8,128)(2,1)} %get-tuple-element.91.grad_ref, f32[16,1024]{1,0:T(8,128)} %get-tuple-element.92.lse_ref, f32[16,1024]{1,0:T(8,128)} %get-tuple-element.93.delta_ref, ...), custom_call_target="tpu_custom_call" | custom-call | flops 1000000 | bytes 100000 | tf_op jit(solution)/shard_map/attend_back/pallas_call | solution.py:1442
  242.2 2.6 concatenate.14.minor_ref
  244.8 7.7 %collective-permute-done.4 = bf16[2,256,768]{2,1,0:T(8,128)(2,1)} collective-permute-done((bf16[2,256,768]{2,1,0:T(8,128)(2,1)}, bf16[2,256,768]{2,1,0:T(8,128)(2,1)}, u32[]{:S(2)}, u32[]{:S(2)}) %collective-permute-start.4) | collective-permute-done | bytes 786464 | tf_op jit(solution)/shard_map/ppermute | solution.py:464
  252.6 3.3 fusion.1.up_ref
  255.9 2.9 fusion.3.pair_ref
  258.8 92.0 %reduce_parts.1 = (f32[12,8,2048]{2,1,0:T(8,128)}, f32[12,8,2048]{2,1,0:T(8,128)}, f32[32,8,768]{2,1,0:T(8,128)}, bf16[24,96,128]{2,1,0:T(8,128)(2,1)}, f32[24,768]{1,0:T(8,128)}) custom-call(bf16[4,12,8,2048]{3,2,1,0:T(8,128)(2,1)} %bitcast.67, bf16[4,12,8,2048]{3,2,1,0:T(8,128)(2,1)} %fusion.1.up_ref, bf16[3,12,8,2048]{3,2,1,0:T(8,128)(2,1)} %bitcast.23.risen_ref, ...), custom_call_target="tpu_custom_call" | custom-call | tf_op jit(solution)/shard_map/reduce_parts/pallas_call | solution.py:939
  350.8 1.2 convert_bitcast_fusion
  352.0 0.9 copy.64
  352.9 0.9 reshape.298
  353.9 1.0 slice.70
  354.8 0.7 slice.71
  355.6 0.6 slice.72
  356.2 0.6 slice.73
  356.8 0.5 slice_bitcast_fusion
  357.3 0.6 slice.74
  357.9 0.6 slice.67
  358.5 1.3 maximum_bitcast_fusion
  359.9 0.9 copy.69
  (69 shorter events, 1.1 us)
Async XLA Ops:
  0.6 3.1 copy-start.20
  0.7 3.1 copy-start.21
  0.7 3.1 copy-start.17
  0.7 3.1 copy-start.18
  0.7 3.1 copy-start.19
  4.5 1.3 copy-start.13
  4.6 2.3 copy-start.11
  4.8 3.6 copy-start.10
  4.8 3.6 copy-start.14
  5.8 3.9 %copy-start.8 = (bf16[96,2304]{1,0:T(8,128)(2,1)S(1)}, bf16[96,2304]{1,0:T(8,128)(2,1)}, u32[]{:S(2)}) copy-start(bf16[96,2304]{1,0:T(8,128)(2,1)} %param.19) | copy-start | bytes 1327108
  5.8 3.9 %copy-start.9 = (bf16[96,768]{1,0:T(8,128)(2,1)S(1)}, bf16[96,768]{1,0:T(8,128)(2,1)}, u32[]{:S(2)}) copy-start(bf16[96,768]{1,0:T(8,128)(2,1)} %param.20) | copy-start | bytes 442372
  147.6 37.6 %collective-permute-start = (bf16[4,96,2048]{2,1,0:T(8,128)(2,1)}, bf16[4,96,2048]{2,1,0:T(8,128)(2,1)}, u32[]{:S(2)}, u32[]{:S(2)}) collective-permute-start(bf16[4,96,2048]{2,1,0:T(8,128)(2,1)} %get-tuple-element.89), channel_id=1, source_target_pairs={{0,4},{4,0},{8,12},{12,8},{16,20},{20,16},{24,28},{28,24},{1,5},{5... | collective-permute-start | bytes 4718600 | tf_op jit(solution)/shard_map/ppermute | solution.py:464
  148.2 104.3 %collective-permute-start.1 = (bf16[4,96,2048]{2,1,0:T(8,128)(2,1)}, bf16[4,96,2048]{2,1,0:T(8,128)(2,1)}, u32[]{:S(2)}, u32[]{:S(2)}) collective-permute-start(bf16[4,96,2048]{2,1,0:T(8,128)(2,1)} %get-tuple-element.102), channel_id=1, source_target_pairs={{0,4},{4,0},{8,12},{12,8},{16,20},{20,16},{24,28},{28,24},{1,5},{5... | collective-permute-start | bytes 4718600 | tf_op jit(solution)/shard_map/ppermute | solution.py:464
  149.7 44.2 %collective-permute-start.2 = (bf16[2,256,768]{2,1,0:T(8,128)(2,1)}, bf16[2,256,768]{2,1,0:T(8,128)(2,1)}, u32[]{:S(2)}, u32[]{:S(2)}) collective-permute-start(bf16[2,256,768]{2,1,0:T(8,128)(2,1)} %get-tuple-element.104), channel_id=1, source_target_pairs={{0,8},{4,12},{8,0},{12,4},{16,24},{20,28},{24,16},{28,20},{1,9},{5... | collective-permute-start | bytes 2359304 | tf_op jit(solution)/shard_map/ppermute | solution.py:464
  152.1 33.2 %copy-start.2 = (bf16[4,96,2048]{2,1,0:T(8,128)(2,1)S(1)}, bf16[4,96,2048]{2,1,0:T(8,128)(2,1)}, u32[]{:S(2)}) copy-start(bf16[4,96,2048]{2,1,0:T(8,128)(2,1)} %get-tuple-element.99) | copy-start | bytes 4718596
  187.3 1.9 copy-start
  187.3 8.1 %copy-start.15 = (f32[8,128]{1,0:T(8,128)S(1)}, f32[8,128]{1,0:T(8,128)}, u32[]{:S(2)}) copy-start(f32[8,128]{1,0:T(8,128)} %get-tuple-element.121) | copy-start | bytes 12292
  187.3 8.9 %copy-start.7 = (f32[1024,8]{1,0:T(8,128)S(1)}, f32[1024,8]{1,0:T(8,128)}, u32[]{:S(2)}) copy-start(f32[1024,8]{1,0:T(8,128)} %get-tuple-element.155) | copy-start | bytes 98308
  189.2 63.3 %collective-permute-start.5 = (bf16[3,96,2048]{2,1,0:T(8,128)(2,1)}, bf16[3,96,2048]{2,1,0:T(8,128)(2,1)}, u32[]{:S(2)}, u32[]{:S(2)}) collective-permute-start(bf16[3,96,2048]{2,1,0:T(8,128)(2,1)} %get-tuple-element.169), channel_id=1, source_target_pairs={{0,8},{4,12},{1,9},{5,13},{2,10},{6,14},{3,11},{7,15}} | collective-permute-start | bytes 3538952 | tf_op jit(solution)/shard_map/ppermute | solution.py:1439
  192.3 60.3 %collective-permute-start.6 = (bf16[3,96,2048]{2,1,0:T(8,128)(2,1)}, bf16[3,96,2048]{2,1,0:T(8,128)(2,1)}, u32[]{:S(2)}, u32[]{:S(2)}) collective-permute-start(bf16[3,96,2048]{2,1,0:T(8,128)(2,1)} %get-tuple-element.168), channel_id=1, source_target_pairs={{24,16},{28,20},{25,17},{29,21},{26,18},{30,22},{27,19},{31,23}} | collective-permute-start | bytes 3538952 | tf_op jit(solution)/shard_map/ppermute | solution.py:1440
  193.9 50.9 %collective-permute-start.3 = (bf16[2,256,768]{2,1,0:T(8,128)(2,1)}, bf16[2,256,768]{2,1,0:T(8,128)(2,1)}, u32[]{:S(2)}, u32[]{:S(2)}) collective-permute-start(bf16[2,256,768]{2,1,0:T(8,128)(2,1)} %get-tuple-element.105), channel_id=1, source_target_pairs={{0,16},{4,20},{8,24},{12,28},{16,0},{20,4},{24,8},{28,12},{1,17},{... | collective-permute-start | bytes 2359304 | tf_op jit(solution)/shard_map/ppermute | solution.py:464
  193.9 58.6 %collective-permute-start.4 = (bf16[2,256,768]{2,1,0:T(8,128)(2,1)}, bf16[2,256,768]{2,1,0:T(8,128)(2,1)}, u32[]{:S(2)}, u32[]{:S(2)}) collective-permute-start(bf16[2,256,768]{2,1,0:T(8,128)(2,1)} %get-tuple-element.106), channel_id=1, source_target_pairs={{0,24},{4,28},{8,16},{12,20},{16,8},{20,12},{24,0},{28,4},{1,25},{... | collective-permute-start | bytes 2359304 | tf_op jit(solution)/shard_map/ppermute | solution.py:464
  197.0 45.2 %copy-start.16 = (f32[1,768]{1,0:T(1,128)S(1)}, f32[1,768]{1,0:T(1,128)}, u32[]{:S(2)}) copy-start(f32[1,768]{1,0:T(1,128)} %get-tuple-element.120) | copy-start | bytes 9220
  197.0 55.6 %copy-start.1 = (bf16[4,96,2048]{2,1,0:T(8,128)(2,1)S(1)}, bf16[4,96,2048]{2,1,0:T(8,128)(2,1)}, u32[]{:S(2)}) copy-start(bf16[4,96,2048]{2,1,0:T(8,128)(2,1)} %get-tuple-element.108) | copy-start | bytes 4718596
  252.6 3.3 copy-start.6
  353.8 1.7 copy-start.12
  353.8 4.7 %copy-start.4 = (f32[12,8,2048]{2,1,0:T(8,128)S(1)}, f32[12,8,2048]{2,1,0:T(8,128)}, u32[]{:S(2)}) copy-start(f32[12,8,2048]{2,1,0:T(8,128)} %get-tuple-element.124) | copy-start | bytes 2359300
  353.9 4.7 %copy-start.5 = (f32[12,8,2048]{2,1,0:T(8,128)S(1)}, f32[12,8,2048]{2,1,0:T(8,128)}, u32[]{:S(2)}) copy-start(f32[12,8,2048]{2,1,0:T(8,128)} %get-tuple-element.125) | copy-start | bytes 2359300
  358.5 1.4 copy-start.3
